TPU v7x, 32 devices: a whole 2x2x4 slice. The times are simulated.
32 devices in a mesh: pipe: 4 (over x, core), mp: 8 (over z, y).
Axes of the slice: x: 2, y: 2, z: 4, core: 2. Of those that a mesh axis runs over, the one named last changes fastest.
Arguments:
- hidden_in: bfloat16 [32, 8192], P(None, 'mp'), may hold values from -24000 to 24000
- lengths: int32 [32], replicated, may hold values from 1 to 256
- assign: int32 [32], replicated, may hold values from 0 to 31, each once
- token_ids: int32 [32], replicated, may hold values from 0 to 12287
- attn_gain: bfloat16 [4, 8192], P('pipe', 'mp'), may hold values from 0.099609375 to 1.8984375
- qkv_weight: bfloat16 [4, 8192, 5120], P('pipe', 'mp'), may hold values from -0.0625 to 0.0625
- qkv_bias: bfloat16 [4, 5120], P('pipe'), may hold values from -3 to 3
- out_weight: bfloat16 [4, 4096, 8192], P('pipe', None, 'mp'), may hold values from -0.375 to 0.375
- kv_cache: bfloat16 [4, 32, 2, 4, 256, 128], P('pipe', 'mp'), may hold values from -120 to 120
- final_gain: bfloat16 [8192], P('mp'), may hold values from 0.099609375 to 1.8984375
- head_weight: bfloat16 [8192, 12288], P(None, ('pipe', 'mp')), may hold values from -0.9923308 to 0.9923308
Outputs:
- logprobs: float32 [32, 12288], P(None, ('pipe', 'mp'))
- chosen: float32 [32], replicated
Inputs may be any that keep to these rules, and one draw needn't show every extreme that they name: `assign`: a permutation of the 32 requests.
All inputs are finite; a program needn't handle non-finite values.
Results may differ from a plain program's by a relative error of at most 0.0017.
Values may be sent and summed in bfloat16 or wider, within the bound.
A program may use at most 64 MiB of HBM per device.

v0:
```python
import functools

import jax
import jax.numpy as jnp
import numpy as np
from jax import lax
from jax.experimental import pallas as pl
from jax.experimental.pallas import tpu as pltpu
from jax.sharding import PartitionSpec as P

HEADS = 32
KV_HEADS = 4
HEAD_DIM = 128
EPS = 1e-06
THETA = 1000000.0
MESH = pl.DeviceIdType.MESH
F32 = jnp.float32
BF16 = jnp.bfloat16


def remote(src, dst, send_sem, recv_sem, device):
    return pltpu.make_async_remote_copy(
        src_ref=src,
        dst_ref=dst,
        send_sem=send_sem,
        recv_sem=recv_sem,
        device_id=device,
        device_id_type=MESH,
    )


def kernel(
    sections,
    n,
    hidden,
    lengths,
    assign,
    token_ids,
    gain,
    qkv_weight,
    bias,
    out_weight,
    cache,
    final_gain,
    head_weight,
    freq,
    out,
    chosen,
    wq,
    wo,
    kv,
    hw,
    x,
    xo,
    scaled,
    stage,
    part,
    part_in,
    sq,
    sq_in,
    bias_rows,
    fresh,
    att,
    att_in,
    update,
    fin,
    fsq_in,
    red,
    red_in,
    wq_sem,
    w_sem,
    part_s,
    part_r,
    sq_s,
    sq_r,
    att_s,
    att_r,
    hop_s,
    hop_r,
    fin_s,
    fin_r,
    sib_s,
    sib_r,
    fsq_s,
    fsq_r,
    fp_s,
    fp_r,
    red_s,
    red_r,
):
    sec = lax.axis_index("pipe")
    me = lax.axis_index("mp")
    total = sections * n
    rows, width = hidden.shape
    lc = kv.shape[0]
    heads_all = HEADS + 2 * KV_HEADS
    group = HEADS // KV_HEADS
    phases = heads_all // group
    span = lc * group
    last = sections - 1
    scale = HEAD_DIM ** (-0.5)
    cw = group * HEAD_DIM
    half = rows // 2
    core = lax.rem(sec, 2)
    sibling = sec + 1 - 2 * core

    def wq_copy(c):
        cols = pl.ds(pl.multiple_of(c * cw, cw), cw)
        return pltpu.make_async_copy(qkv_weight.at[0, :, cols], wq.at[:, cols], wq_sem.at[c])

    def phase_of(k):
        return lax.rem(k + phases - 1, phases)

    for k in range(phases):
        wq_copy((k + phases - 1) % phases).start()
    kv_copy = pltpu.make_async_copy(cache.at[0], kv, w_sem.at[0])
    wo_copy = pltpu.make_async_copy(out_weight.at[0], wo, w_sem.at[1])
    hw_copy = pltpu.make_async_copy(head_weight, hw, w_sem.at[2])

    @pl.when(sec > 0)
    def _():
        kv_copy.start()
        wo_copy.start()
        hw_copy.start()

    barrier = pltpu.get_barrier_semaphore()
    mine = sec * n + me

    def greet(k, carry):
        other = lax.rem(mine + k, total)
        pl.semaphore_signal(
            barrier, inc=1, device_id=(other // n, lax.rem(other, n)), device_id_type=MESH
        )
        return carry

    lax.fori_loop(1, total, greet, 0)

    for i in range(heads_all):
        bias_rows[i : i + 1, :] = bias[:, i * HEAD_DIM : (i + 1) * HEAD_DIM].astype(F32)
    eye = lax.broadcasted_iota(jnp.int32, (rows, 128), 0) == lax.broadcasted_iota(
        jnp.int32, (rows, 128), 1
    )

    def to_row(col):
        return jnp.sum(jnp.where(eye, col, 0.0), axis=0, keepdims=True)

    def to_col(row):
        return jnp.sum(jnp.where(eye, row, 0.0), axis=1, keepdims=True)

    small_eye = lax.broadcasted_iota(jnp.int32, (rows, rows), 0) == lax.broadcasted_iota(
        jnp.int32, (rows, rows), 1
    )
    assign_col = jnp.sum(
        jnp.where(small_eye, assign[...].astype(F32), 0.0), axis=1, keepdims=True
    )
    order = assign_col == lax.broadcasted_iota(jnp.int32, (rows, rows), 1).astype(F32)
    target = jnp.sum(
        jnp.where(order, token_ids[...].astype(F32), 0.0), axis=1, keepdims=True
    )
    lane = lax.broadcasted_iota(jnp.int32, (1, HEAD_DIM), 1)
    lane_rows = lax.broadcasted_iota(jnp.int32, (1, rows), 1)
    own_len = [
        jnp.sum(
            jnp.where(lane_rows == me * lc + i, lengths[...].astype(F32), 0.0),
            axis=1,
            keepdims=True,
        )
        for i in range(lc)
    ]
    angles = jnp.concatenate([length * freq[...] for length in own_len], axis=0)
    cosine = jnp.cos(angles)
    sine = jnp.sin(angles) * jnp.where(lane < HEAD_DIM // 2, -1.0, 1.0)

    pl.semaphore_wait(barrier, total - 1)

    @pl.when(sec == 0)
    def _():
        x[...] = hidden[...]

    @pl.when(sec > 0)
    def _():
        remote(xo, x, hop_s, hop_r, (sec - 1, me)).wait_recv()

    current = x[...].astype(F32)
    sq[...] = jnp.broadcast_to(
        to_row(jnp.sum(current * current, axis=1, keepdims=True)), sq.shape
    )
    scaled[...] = (current * gain[...].astype(F32)).astype(BF16)

    def sq_copy(peer, slot):
        return remote(sq, sq_in.at[slot], sq_s.at[peer], sq_r.at[slot], (sec, peer))

    def to_peer(k):
        return lax.rem(me + k, n)

    for k in range(1, n):
        sq_copy(to_peer(k), me).start()
    sq_in[me] = sq[...]

    def part_copy(phase, peer, slot):
        return remote(
            part.at[phase, peer],
            part_in.at[phase, slot],
            part_s.at[phase, peer],
            part_r.at[phase, slot],
            (sec, peer),
        )

    def project(k, carry):
        phase = phase_of(k)
        wq_copy(phase).wait()
        base = pl.multiple_of(phase * cw, cw)
        piece = jnp.dot(scaled[...], wq[:, pl.ds(base, cw)], preferred_element_type=F32)
        for j in range(group):
            stage[pl.ds(j, rows, stride=group), :] = piece[
                :, j * HEAD_DIM : (j + 1) * HEAD_DIM
            ]
        for p in range(n):
            part[phase, p] = stage[p * span : (p + 1) * span, :].astype(BF16)
        for k in range(1, n):
            part_copy(phase, to_peer(k), me).start()
        part_in[phase, me] = part[phase, me]
        return carry

    lax.fori_loop(0, phases, project, 0)

    @pl.when(sec == 0)
    def _():
        kv_copy.start()
        wo_copy.start()
        hw_copy.start()

    def from_peer(k):
        return lax.rem(me + n - k, n)

    def summed(phase):
        for k in range(1, n):
            peer = from_peer(k)
            part_copy(phase, peer, peer).wait_recv()
        result = part_in[phase, 0].astype(F32)
        for p in range(1, n):
            result = result + part_in[phase, p].astype(F32)
        return result

    for k in range(1, n):
        peer = from_peer(k)
        sq_copy(peer, peer).wait_recv()
    squares = sq_in[0]
    for p in range(1, n):
        squares = squares + sq_in[p]
    factor = [
        lax.rsqrt(
            jnp.sum(
                jnp.where(lane == me * lc + i, squares[0:1, :], 0.0), axis=1, keepdims=True
            )
            / (n * width)
            + EPS
        )
        for i in range(lc)
    ]

    def turn(block, i):
        return (
            block * cosine[i : i + 1]
            + pltpu.roll(block, HEAD_DIM // 2, 1) * sine[i : i + 1]
        )

    is_key = lax.broadcasted_iota(jnp.int32, (2 * KV_HEADS, HEAD_DIM), 0) < KV_HEADS
    block_sum = summed(phases - 1)
    for i in range(lc):
        block = block_sum[i * group : (i + 1) * group] * factor[i] + bias_rows[HEADS:, :]
        fresh[i] = jnp.where(is_key, turn(block, i), block).astype(BF16).astype(F32)
    kv_copy.wait()
    pos = lax.broadcasted_iota(jnp.int32, (1, kv.shape[3]), 1).astype(F32)

    def att_copy(h, peer, slot):
        return remote(
            att.at[h], att_in.at[h, slot], att_s.at[h, peer], att_r.at[h, slot], (sec, peer)
        )

    def attend(h, carry):
        block_sum = summed(h)
        bias_h = bias_rows[pl.ds(pl.multiple_of(h * group, group), group), :]
        done = []
        for i in range(lc):
            block = block_sum[i * group : (i + 1) * group] * factor[i] + bias_h
            query = turn(block, i).astype(BF16)
            key_new = fresh[i, pl.ds(h, 1), :]
            value_new = fresh[i, pl.ds(KV_HEADS + h, 1), :]
            visible = pos < own_len[i]
            scores = (
                lax.dot_general(
                    query,
                    kv[i, 0, h],
                    (((1,), (1,)), ((), ())),
                    preferred_element_type=F32,
                )
                * scale
            )
            self_score = (
                jnp.sum(query.astype(F32) * key_new, axis=1, keepdims=True) * scale
            )
            top = jnp.maximum(
                jnp.max(jnp.where(visible, scores, -1e30), axis=1, keepdims=True), self_score
            )
            weights = jnp.where(visible, jnp.exp(scores - top), 0.0)
            self_weight = jnp.exp(self_score - top)
            denominator = jnp.sum(weights, axis=1, keepdims=True) + self_weight
            mixed = jnp.dot(weights.astype(BF16), kv[i, 1, h], preferred_element_type=F32)
            mixed = mixed + self_weight.astype(BF16).astype(F32) * value_new
            done.append(mixed / denominator)
        att[h] = jnp.concatenate(done, axis=0).astype(BF16)
        for k in range(1, n):
            att_copy(h, to_peer(k), me).start()
        att_in[h, me] = att[h]
        return carry

    lax.fori_loop(0, KV_HEADS, attend, 0)
    wo_copy.wait()
    update[...] = x[...].astype(F32)

    def project_out(h, carry):
        for k in range(1, n):
            peer = from_peer(k)
            att_copy(h, peer, peer).wait_recv()
        for p in range(n):
            stage[p * span : (p + 1) * span, :] = att_in[h, p].astype(F32)
        mat = jnp.concatenate(
            [stage[pl.ds(j, rows, stride=group), :].astype(BF16) for j in range(group)],
            axis=1,
        )
        depth = pl.ds(pl.multiple_of(h * cw, cw), cw)
        update[...] += jnp.dot(mat, wo[depth, :], preferred_element_type=F32)
        return carry

    lax.fori_loop(0, KV_HEADS, project_out, 0)
    xo[...] = update[...].astype(BF16)

    @pl.when(sec < last)
    def _():
        hop = remote(xo, x, hop_s, hop_r, (sec + 1, me))
        hop.start()
        hop.wait_send()

    def fin_pipe(k):
        to = lax.rem(sec + k, sections)
        piece = lax.rem(to, 2)
        return (
            remote(fin.at[piece, me], fin.at[piece, me], fp_s.at[2 * k], fp_r.at[0], (to, me)),
            remote(fsq_in.at[me], fsq_in.at[me], fp_s.at[2 * k + 1], fp_r.at[1], (to, me)),
        )

    @pl.when(sec == last)
    def _():
        final = jnp.dot(order.astype(BF16), xo[...], preferred_element_type=F32)
        both = (final * final_gain[...].astype(F32)).astype(BF16)
        fin[0, me] = both[:half]
        fin[1, me] = both[half:]
        fsq_in[me] = jnp.broadcast_to(
            to_row(jnp.sum(final * final, axis=1, keepdims=True)), (8, 128)
        )
        for k in range(1, sections):
            for copy in fin_pipe(k):
                copy.start()

    @pl.when(sec < last)
    def _():
        arriving = remote(fin.at[core, me], fin.at[core, me], fp_s.at[0], fp_r.at[0], (last, me))
        arriving.wait_recv()
        arriving = remote(fsq_in.at[me], fsq_in.at[me], fp_s.at[1], fp_r.at[1], (last, me))
        arriving.wait_recv()

    def fin_copy(peer, slot):
        return remote(
            fin.at[core, slot], fin.at[core, slot], fin_s.at[peer], fin_r.at[slot], (sec, peer)
        )

    def sib_copy(piece, slot):
        return remote(
            fin.at[piece, slot], fin.at[piece, slot], sib_s.at[slot], sib_r.at[slot], (sibling, me)
        )

    def fsq_copy(peer, slot):
        return remote(
            fsq_in.at[slot], fsq_in.at[slot], fsq_s.at[peer], fsq_r.at[slot], (sec, peer)
        )

    for k in range(1, n):
        fin_copy(to_peer(k), me).start()
    for k in range(1, n):
        fsq_copy(to_peer(k), me).start()

    @pl.when(sec < last - 1)
    def _():
        sib_copy(core, me).start()

    @pl.when(sec == last - 1)
    def _():
        mate = remote(fin.at[1 - core, me], fin.at[1 - core, me], fp_s.at[0], fp_r.at[2], (last, me))
        mate.wait_recv()

    @pl.when(sec == last)
    def _():
        mate = remote(
            fin.at[core, me], fin.at[core, me], sib_s.at[me], fp_r.at[2], (sibling, me)
        )
        mate.start()

    for k in range(1, n):
        peer = from_peer(k)
        fin_copy(peer, peer).wait_recv()
        sib_copy(core, peer).start()

    @pl.when(sec < last - 1)
    def _():
        sib_copy(1 - core, me).wait_recv()

    hw_copy.wait()

    def head(k, logits):
        peer = from_peer(k)

        @pl.when(k > 0)
        def _():
            sib_copy(1 - core, peer).wait_recv()

        rows_at = pl.ds(pl.multiple_of(peer * width, width), width)
        both = jnp.concatenate([fin[0, peer], fin[1, peer]], axis=0)
        return logits + jnp.dot(both, hw[rows_at, :], preferred_element_type=F32)

    logits = lax.fori_loop(0, n, head, jnp.zeros(out.shape, F32))
    for k in range(1, n):
        peer = from_peer(k)
        fsq_copy(peer, peer).wait_recv()
    squares = fsq_in[0]
    for p in range(1, n):
        squares = squares + fsq_in[p]
    logits = logits * lax.rsqrt(to_col(squares[0:1, :]) / (n * width) + EPS)
    vocab = out.shape[1]
    ids = (mine * vocab + lax.broadcasted_iota(jnp.int32, (1, vocab), 1)).astype(F32)
    picked = jnp.sum(jnp.where(ids == target, logits, 0.0), axis=1, keepdims=True)
    top = jnp.max(logits, axis=1, keepdims=True)
    amount = jnp.sum(jnp.exp(logits - top), axis=1, keepdims=True)
    red[...] = jnp.concatenate(
        [to_row(top), to_row(amount), to_row(picked), jnp.zeros((5, 128), F32)], axis=0
    )

    def red_copy(other, slot):
        return remote(
            red,
            red_in.at[slot],
            red_s.at[other],
            red_r.at[slot],
            (other // n, lax.rem(other, n)),
        )

    def red_start(k, carry):
        red_copy(lax.rem(mine + k, total), mine).start()
        return carry

    lax.fori_loop(1, total, red_start, 0)
    red_in[mine] = red[...]

    def red_wait(k, carry):
        other = lax.rem(mine + total - k, total)
        red_copy(other, other).wait_recv()
        return carry

    lax.fori_loop(1, total, red_wait, 0)
    tops = red_in[:, 0, :]
    row_top = jnp.max(tops, axis=0, keepdims=True)
    row_total = jnp.sum(red_in[:, 1, :] * jnp.exp(tops - row_top), axis=0, keepdims=True)
    log_total = row_top + jnp.log(row_total)
    chosen[...] = jnp.sum(red_in[:, 2, :], axis=0, keepdims=True) - log_total
    out[...] = logits - to_col(log_total)

    def peer_done(k, carry):
        peer = to_peer(k)
        sq_copy(peer, me).wait_send()
        for phase in range(phases):
            part_copy(phase, peer, me).wait_send()
        for h in range(KV_HEADS):
            att_copy(h, peer, me).wait_send()
        fin_copy(peer, me).wait_send()
        fsq_copy(peer, me).wait_send()
        sib_copy(core, peer).wait_send()
        return carry

    lax.fori_loop(1, n, peer_done, 0)

    @pl.when(sec != last - 1)
    def _():
        sib_copy(core, me).wait_send()

    @pl.when(sec == last)
    def _():
        for k in range(1, sections):
            for copy in fin_pipe(k):
                copy.wait_send()

    def red_done(k, carry):
        red_copy(lax.rem(mine + k, total), mine).wait_send()
        return carry

    lax.fori_loop(1, total, red_done, 0)


def local(
    hidden_in,
    lengths,
    assign,
    token_ids,
    attn_gain,
    qkv_weight,
    qkv_bias,
    out_weight,
    kv_cache,
    final_gain,
    head_weight,
):
    sections = lax.axis_size("pipe")
    n = lax.axis_size("mp")
    rows, width = hidden_in.shape
    lc = kv_cache.shape[1]
    qkv = qkv_weight.shape[2]
    inner = out_weight.shape[1]
    vocab = head_weight.shape[1]
    heads_all = HEADS + 2 * KV_HEADS
    half = HEAD_DIM // 2
    frequency = np.float32(THETA) ** (
        -np.arange(half).astype(np.float32) * np.float32(2.0) / np.float32(HEAD_DIM)
    )
    freq = jnp.asarray(np.concatenate([frequency, frequency])[None, :], F32)
    group = HEADS // KV_HEADS
    phases = heads_all // group
    span = lc * group
    dma = pltpu.SemaphoreType.DMA
    vm = pl.BlockSpec(memory_space=pltpu.VMEM)
    hbm = pl.BlockSpec(memory_space=pl.ANY)
    total = sections * n
    logprobs, chosen = pl.pallas_call(
        functools.partial(kernel, sections, n),
        out_shape=(
            jax.ShapeDtypeStruct((rows, vocab), F32),
            jax.ShapeDtypeStruct((1, 128), F32),
        ),
        in_specs=[vm, vm, vm, vm, vm, hbm, vm, hbm, hbm, vm, hbm, vm],
        out_specs=(vm, vm),
        scratch_shapes=[
            pltpu.VMEM((width, qkv), BF16),
            pltpu.VMEM((inner, width), BF16),
            pltpu.VMEM(kv_cache.shape[1:], BF16),
            pltpu.VMEM(head_weight.shape, BF16),
            pltpu.VMEM((rows, width), BF16),
            pltpu.VMEM((rows, width), BF16),
            pltpu.VMEM((rows, width), BF16),
            pltpu.VMEM((rows * group, HEAD_DIM), F32),
            pltpu.VMEM((phases, n, span, HEAD_DIM), BF16),
            pltpu.VMEM((phases, n, span, HEAD_DIM), BF16),
            pltpu.VMEM((8, 128), F32),
            pltpu.VMEM((n, 8, 128), F32),
            pltpu.VMEM((heads_all, HEAD_DIM), F32),
            pltpu.VMEM((lc, 2 * KV_HEADS, HEAD_DIM), F32),
            pltpu.VMEM((KV_HEADS, span, HEAD_DIM), BF16),
            pltpu.VMEM((KV_HEADS, n, span, HEAD_DIM), BF16),
            pltpu.VMEM((rows, width), F32),
            pltpu.VMEM((2, n, rows // 2, width), BF16),
            pltpu.VMEM((n, 8, 128), F32),
            pltpu.VMEM((8, 128), F32),
            pltpu.VMEM((total, 8, 128), F32),
            dma((phases,)),
            dma((3,)),
            dma((phases, n)),
            dma((phases, n)),
            dma((n,)),
            dma((n,)),
            dma((KV_HEADS, n)),
            dma((KV_HEADS, n)),
            dma,
            dma,
            dma((n,)),
            dma((n,)),
            dma((n,)),
            dma((n,)),
            dma((n,)),
            dma((n,)),
            dma((2 * sections,)),
            dma((3,)),
            dma((total,)),
            dma((total,)),
        ],
        compiler_params=pltpu.CompilerParams(
            collective_id=0, has_side_effects=True, vmem_limit_bytes=60 * 1024 * 1024
        ),
    )(
        hidden_in,
        lengths.reshape(1, rows),
        assign.reshape(1, rows),
        token_ids.reshape(1, rows),
        attn_gain,
        qkv_weight,
        qkv_bias,
        out_weight,
        kv_cache,
        final_gain.reshape(1, width),
        head_weight,
        freq,
    )
    return logprobs, chosen[0, :rows]


def solution(mesh):
    return jax.shard_map(
        local,
        mesh=mesh,
        in_specs=(
            P(None, "mp"),
            P(),
            P(),
            P(),
            P("pipe", "mp"),
            P("pipe", "mp", None),
            P("pipe", None),
            P("pipe", None, "mp"),
            P("pipe", "mp", None, None, None, None),
            P("mp"),
            P(None, ("pipe", "mp")),
        ),
        out_specs=(P(None, ("pipe", "mp")), P()),
        check_vma=False,
    )
```

profile of v0, /device:TPU:0, one launch (start us, length us, event | category | flops | bytes accessed | tf_op | source)
XLA Modules:
  0.0 95.1 jit_solution(14895891834392191745)
XLA Ops:
  0.6 1.3 %reshape.19.final_gain = bf16[1,1024]{1,0:T(2,128)(2,1)} reshape(bf16[1024]{0:T(1024)(128)(2,1)} %param.21) | data formatting | bytes 4096 | tf_op jit(solution)/shard_map/reshape | solution.py:605
  1.9 90.6 %shard_map.131 = (f32[32,384]{1,0:T(8,128)}, f32[1,128]{1,0:T(1,128)}) custom-call(bf16[32,1024]{1,0:T(8,128)(2,1)} %hidden.1, s32[1,32]{1,0:T(1,128)} %bitcast.5, s32[1,32]{1,0:T(1,128)} %bitcast.6, s32[1,32]{1,0:T(1,128)} %bitcast.7, bf16[1,1024]{1,0:T(2,128)(2,1)} %gain.1, bf16[1,1024,5120]{2,1,0:T(8,128)(2,1)} %qkv_weight.1, bf16[1,5120]{1,0:T(2,128)(2,1)} %bias.1, ...), custom_call_target="tpu_custom_call" | custom-call | tf_op jit(solution)/shard_map/pallas_call | solution.py:541
  92.5 1.1 %slice_bitcast_fusion = f32[32]{0:T(128)} fusion(f32[1,128]{1,0:T(1,128)} %get-tuple-element.5), kind=kLoop, calls=%fused_computation | loop fusion | bytes 256 | tf_op jit(solution)/shard_map/squeeze | solution.py:609
  93.6 1.4 %copy.15 = f32[32,384]{1,0:T(8,128)} copy(f32[32,384]{1,0:T(8,128)} %get-tuple-element.8) | data formatting | bytes 98304
where the time goes:
time: 95.3 us; the launch traced here: 95.1 us
  Pallas kernels  90.6 us (95%)
  local copies, waits for them, and re-layouts  3.84 us (4%)
    pallas_call x1, Pallas kernels, local(): pl.pallas_call(functools.partial(kernel, sections, n), out_shape=(jax.Sha...  90.6 us

commit v1 on v0

v1 whole, which is shorter than its diff:
```python
import functools

import jax
import jax.numpy as jnp
import numpy as np
from jax import lax
from jax.experimental import pallas as pl
from jax.experimental.pallas import tpu as pltpu
from jax.sharding import PartitionSpec as P

HEADS = 32
KV_HEADS = 4
HEAD_DIM = 128
EPS = 1e-06
THETA = 1000000.0
MESH = pl.DeviceIdType.MESH
F32 = jnp.float32
BF16 = jnp.bfloat16


def remote(src, dst, send_sem, recv_sem, device):
    return pltpu.make_async_remote_copy(
        src_ref=src,
        dst_ref=dst,
        send_sem=send_sem,
        recv_sem=recv_sem,
        device_id=device,
        device_id_type=MESH,
    )


def kernel(
    sections,
    n,
    hidden,
    lengths,
    assign,
    token_ids,
    gain,
    qkv_weight,
    bias,
    out_weight,
    cache,
    final_gain,
    head_weight,
    freq,
    out,
    chosen,
    wq,
    wo,
    kv,
    hw,
    x,
    xo,
    scaled,
    stage,
    part,
    part_in,
    sq,
    sq_in,
    gain_v,
    bias_v,
    final_v,
    len_v,
    slot_v,
    token_v,
    freq_v,
    slot_s,
    bias_rows,
    turn_cos,
    turn_sin,
    own_rows,
    target_v,
    fresh,
    att,
    att_in,
    update,
    fin,
    fsq_in,
    red,
    red_in,
    flat,
    wq_sem,
    w_sem,
    small_sem,
    part_s,
    part_r,
    sq_s,
    sq_r,
    att_s,
    att_r,
    hop_s,
    hop_r,
    fin_s,
    fin_r,
    sib_s,
    sib_r,
    fsq_s,
    fsq_r,
    fp_s,
    fq_s,
    fp_r,
    red_s,
    red_r,
):
    sec = lax.axis_index("pipe")
    me = lax.axis_index("mp")
    total = sections * n
    rows, width = x.shape
    lc = kv.shape[0]
    heads_all = HEADS + 2 * KV_HEADS
    group = HEADS // KV_HEADS
    phases = heads_all // group
    span = lc * group
    last = sections - 1
    scale = HEAD_DIM ** (-0.5)
    cw = group * HEAD_DIM
    half = rows // 2
    chunks = fin.shape[2]
    chunk = width // chunks
    core = lax.rem(sec, 2)
    sibling = sec + 1 - 2 * core
    mine = sec * n + me
    early = min(2, phases)

    def mate(own, k, count):
        if count & (count - 1):
            return lax.rem(own + k, count), lax.rem(own + count - k, count)
        other = 0
        for b in range(count.bit_length() - 1):
            place = 1 << b
            mine_bit = lax.rem(own // place, 2)
            if isinstance(k, int):
                bit = 1 - mine_bit if (k // place) % 2 else mine_bit
            else:
                flip = lax.rem(k // place, 2)
                bit = mine_bit + flip - 2 * mine_bit * flip
            other = other + place * bit
        return other, other

    pairs = [mate(me, k, n) for k in range(n)]
    far_first = range(n - 1, 0, -1)

    def to_peer(k):
        return pairs[k][0]

    def from_peer(k):
        return pairs[k][1]

    def wq_copy(c):
        cols = pl.ds(pl.multiple_of(c * cw, cw), cw)
        return pltpu.make_async_copy(qkv_weight.at[0, :, cols], wq.at[:, cols], wq_sem.at[c])

    def phase_of(k):
        return lax.rem(k + phases - 1, phases)

    def small(i, src, dst):
        return pltpu.make_async_copy(src, dst, small_sem.at[i])

    hidden_copy = small(0, hidden, x)
    gain_copy = small(1, gain, gain_v)
    others = [
        small(2, bias, bias_v),
        small(3, final_gain, final_v),
        small(4, lengths, len_v),
        small(5, assign, slot_v),
        small(6, token_ids, token_v),
        small(7, freq, freq_v),
        small(8, assign, slot_s),
    ]

    @pl.when(sec == 0)
    def _():
        hidden_copy.start()

    gain_copy.start()
    for k in range(early):
        wq_copy((k + phases - 1) % phases).start()

    def wq_rest():
        for k in range(early, phases):
            wq_copy((k + phases - 1) % phases).start()

    kv_copy = pltpu.make_async_copy(cache.at[0], kv, w_sem.at[0])
    wo_copy = pltpu.make_async_copy(out_weight.at[0], wo, w_sem.at[1])
    hw_copy = pltpu.make_async_copy(head_weight, hw, w_sem.at[2])

    barrier = pltpu.get_barrier_semaphore()
    for k in far_first:
        pl.semaphore_signal(barrier, inc=1, device_id=(sec, to_peer(k)), device_id_type=MESH)
    for k in range(1, sections):
        pl.semaphore_signal(
            barrier, inc=1, device_id=(lax.rem(sec + k, sections), me), device_id_type=MESH
        )
    @pl.when(sec > 0)
    def _():
        for copy in others:
            copy.start()
        wq_rest()
        kv_copy.start()
        wo_copy.start()
        hw_copy.start()

    eye = lax.broadcasted_iota(jnp.int32, (rows, 128), 0) == lax.broadcasted_iota(
        jnp.int32, (rows, 128), 1
    )

    def to_row(col):
        return jnp.sum(jnp.where(eye, col, 0.0), axis=0, keepdims=True)

    def to_col(row):
        return jnp.sum(jnp.where(eye, row, 0.0), axis=1, keepdims=True)

    lane = lax.broadcasted_iota(jnp.int32, (1, HEAD_DIM), 1)
    lane_rows = lax.broadcasted_iota(jnp.int32, (1, rows), 1)
    small_eye = lax.broadcasted_iota(jnp.int32, (rows, rows), 0) == lax.broadcasted_iota(
        jnp.int32, (rows, rows), 1
    )

    def set_up():
        for copy in others:
            copy.wait()
        for i in range(heads_all):
            bias_rows[i : i + 1, :] = bias_v[:, i * HEAD_DIM : (i + 1) * HEAD_DIM].astype(F32)
        target = jnp.sum(
            jnp.where(small_eye, token_v[...].astype(F32), 0.0), axis=1, keepdims=True
        )
        target_v[...] = jnp.broadcast_to(target, target_v.shape)
        for i in range(lc):
            length = jnp.sum(
                jnp.where(lane_rows == me * lc + i, len_v[...].astype(F32), 0.0),
                axis=1,
                keepdims=True,
            )
            own_rows[i : i + 1, :] = jnp.broadcast_to(length, (1, HEAD_DIM))
        angles = own_rows[...] * freq_v[...]
        turn_cos[...] = jnp.cos(angles)
        turn_sin[...] = jnp.sin(angles) * jnp.where(lane < HEAD_DIM // 2, -1.0, 1.0)

    def scale_rows():
        gain_copy.wait()
        current = x[...].astype(F32)
        sq[...] = jnp.broadcast_to(
            to_row(jnp.sum(current * current, axis=1, keepdims=True)), sq.shape
        )
        scaled[...] = (current * gain_v[...].astype(F32)).astype(BF16)

    def sq_copy(peer, slot):
        return remote(sq, sq_in.at[slot], sq_s, sq_r, (sec, peer))

    def sq_send():
        for k in far_first:
            sq_copy(to_peer(k), me).start()
        sq_in[me] = sq[...]

    def part_copy(phase, peer, slot):
        return remote(
            part.at[phase, peer],
            part_in.at[phase, slot],
            part_s,
            part_r.at[phase],
            (sec, peer),
        )

    def multiply(phase):
        wq_copy(phase).wait()
        base = pl.multiple_of(phase * cw, cw)
        piece = jnp.dot(scaled[...], wq[:, pl.ds(base, cw)], preferred_element_type=F32)
        for j in range(group):
            stage[pl.ds(j, rows, stride=group), :] = piece[
                :, j * HEAD_DIM : (j + 1) * HEAD_DIM
            ]
        for p in range(n):
            part[phase, p] = stage[p * span : (p + 1) * span, :].astype(BF16)

    def spread(phase):
        for k in far_first:
            part_copy(phase, to_peer(k), me).start()
        part_in[phase, me] = part[phase, me]

    def compute_only(k, carry):
        multiply(phase_of(k))
        return carry

    def send_only(k, carry):
        spread(phase_of(k))
        return carry

    def project(k, carry):
        multiply(phase_of(k))
        spread(phase_of(k))
        return carry

    def hop_copy(c, to):
        cols = pl.ds(c * chunk, chunk)
        return remote(xo.at[:, cols], x.at[:, cols], hop_s, hop_r, (to, me))


    @pl.when(sec == 0)
    def _():
        hidden_copy.wait()
        scale_rows()
        wq_rest()
        for copy in others:
            copy.start()
        lax.fori_loop(0, early, compute_only, 0)

    @pl.when(sec > 0)
    def _():
        set_up()

    pl.semaphore_wait(barrier, n + sections - 2)

    @pl.when(sec == 0)
    def _():
        sq_send()
        lax.fori_loop(0, early, send_only, 0)

    @pl.when(sec > 0)
    def _():
        remote(xo, x, hop_s, hop_r, (sec - 1, me)).wait_recv()
        scale_rows()
        sq_send()

    lax.fori_loop(jnp.where(sec == 0, early, 0), phases, project, 0)

    @pl.when(sec == 0)
    def _():
        kv_copy.start()
        wo_copy.start()
        hw_copy.start()
        set_up()

    def summed(phase):
        remote(
            part.at[phase, pl.ds(1, n - 1)],
            part_in.at[phase, pl.ds(1, n - 1)],
            part_s,
            part_r.at[phase],
            (sec, me),
        ).wait_recv()
        result = part_in[phase, 0].astype(F32)
        for p in range(1, n):
            result = result + part_in[phase, p].astype(F32)
        return result

    remote(
        sq_in.at[pl.ds(1, n - 1)], sq_in.at[pl.ds(1, n - 1)], sq_s, sq_r, (sec, me)
    ).wait_recv()
    squares = sq_in[0]
    for p in range(1, n):
        squares = squares + sq_in[p]
    factor = [
        lax.rsqrt(
            jnp.sum(
                jnp.where(lane == me * lc + i, squares[0:1, :], 0.0), axis=1, keepdims=True
            )
            / (n * width)
            + EPS
        )
        for i in range(lc)
    ]
    own_len = [own_rows[i : i + 1, 0:1] for i in range(lc)]
    cosine = turn_cos[...]
    sine = turn_sin[...]

    def turn(block, i):
        return (
            block * cosine[i : i + 1]
            + pltpu.roll(block, HEAD_DIM // 2, 1) * sine[i : i + 1]
        )

    is_key = lax.broadcasted_iota(jnp.int32, (2 * KV_HEADS, HEAD_DIM), 0) < KV_HEADS
    block_sum = summed(phases - 1)
    for i in range(lc):
        block = block_sum[i * group : (i + 1) * group] * factor[i] + bias_rows[HEADS:, :]
        fresh[i] = jnp.where(is_key, turn(block, i), block).astype(BF16).astype(F32)
    kv_copy.wait()
    pos = lax.broadcasted_iota(jnp.int32, (1, kv.shape[3]), 1).astype(F32)

    def att_copy(h, peer, slot):
        return remote(
            att.at[h], att_in.at[h, slot], att_s, att_r.at[h], (sec, peer)
        )

    def attend(h, carry):
        block_sum = summed(h)
        bias_h = bias_rows[pl.ds(pl.multiple_of(h * group, group), group), :]
        done = []
        for i in range(lc):
            block = block_sum[i * group : (i + 1) * group] * factor[i] + bias_h
            query = turn(block, i).astype(BF16)
            key_new = fresh[i, pl.ds(h, 1), :]
            value_new = fresh[i, pl.ds(KV_HEADS + h, 1), :]
            visible = pos < own_len[i]
            scores = (
                lax.dot_general(
                    query,
                    kv[i, 0, h],
                    (((1,), (1,)), ((), ())),
                    preferred_element_type=F32,
                )
                * scale
            )
            self_score = (
                jnp.sum(query.astype(F32) * key_new, axis=1, keepdims=True) * scale
            )
            top = jnp.maximum(
                jnp.max(jnp.where(visible, scores, -1e30), axis=1, keepdims=True), self_score
            )
            weights = jnp.where(visible, jnp.exp(scores - top), 0.0)
            self_weight = jnp.exp(self_score - top)
            denominator = jnp.sum(weights, axis=1, keepdims=True) + self_weight
            mixed = jnp.dot(weights.astype(BF16), kv[i, 1, h], preferred_element_type=F32)
            mixed = mixed + self_weight.astype(BF16).astype(F32) * value_new
            done.append(mixed / denominator)
        att[h] = jnp.concatenate(done, axis=0).astype(BF16)
        for k in far_first:
            att_copy(h, to_peer(k), me).start()
        att_in[h, me] = att[h]
        return carry

    lax.fori_loop(0, KV_HEADS, attend, 0)
    wo_copy.wait()
    update[...] = x[...].astype(F32)

    def all_att(h):
        return remote(
            att_in.at[h, pl.ds(1, n - 1)],
            att_in.at[h, pl.ds(1, n - 1)],
            att_s,
            att_r.at[h],
            (sec, me),
        )

    def gathered(h):
        all_att(h).wait_recv()
        for p in range(n):
            stage[p * span : (p + 1) * span, :] = att_in[h, p].astype(F32)
        return jnp.concatenate(
            [stage[pl.ds(j, rows, stride=group), :].astype(BF16) for j in range(group)],
            axis=1,
        )

    def project_out(h, carry):
        mat = gathered(h)
        depth = pl.ds(pl.multiple_of(h * cw, cw), cw)
        update[...] += jnp.dot(mat, wo[depth, :], preferred_element_type=F32)
        return carry

    lax.fori_loop(0, KV_HEADS - 1, project_out, 0)

    def fin_copy(c, peer, slot):
        return remote(
            fin.at[core, slot, c],
            fin.at[core, slot, c],
            fin_s,
            fin_r.at[slot],
            (sec, peer),
        )

    def sib_copy(c, piece, slot):
        return remote(
            fin.at[piece, slot, c],
            fin.at[piece, slot, c],
            sib_s,
            sib_r.at[slot],
            (sibling, me),
        )

    def fsq_copy(peer, slot):
        return remote(
            fsq_in.at[slot], fsq_in.at[slot], fsq_s, fsq_r, (sec, peer)
        )

    def fp_copy(c, k):
        to = lax.rem(sec + k, sections)
        piece = lax.rem(to, 2)
        return remote(
            fin.at[piece, me, c], fin.at[piece, me, c], fp_s, fp_r.at[c], (to, me)
        )

    def fp_sq(k):
        to = lax.rem(sec + k, sections)
        return remote(
            fsq_in.at[me], fsq_in.at[me], fq_s, fp_r.at[chunks], (to, me)
        )

    mat = gathered(KV_HEADS - 1)
    top_rows = (KV_HEADS - 1) * cw
    final_sq = jnp.zeros((rows, 1), F32)
    for c in range(chunks):
        cols = slice(c * chunk, (c + 1) * chunk)
        grown = update[:, cols] + jnp.dot(
            mat, wo[top_rows : top_rows + cw, cols], preferred_element_type=F32
        )
        new = grown.astype(BF16)
        xo[:, cols] = new
        final = new.astype(F32)
        final_sq = final_sq + jnp.sum(final * final, axis=1, keepdims=True)

        @pl.when(sec < last)
        def _():
            hop_copy(c, sec + 1).start()

        @pl.when(sec == last)
        def _():
            lanes = chunk // 128
            row = jnp.concatenate(
                [final_v[c * lanes + i : c * lanes + i + 1, :].astype(F32) for i in range(lanes)],
                axis=1,
            )
            both = (final * row).astype(BF16)
            fin[0, me, c] = both[:half]
            fin[1, me, c] = both[half:]
            for k in range(1, sections):
                fp_copy(c, k).start()
            for k in far_first:
                fin_copy(c, to_peer(k), me).start()
            sib_copy(c, core, me).start()

    @pl.when(sec == last)
    def _():
        fsq_in[me] = to_row(final_sq)
        for k in range(1, sections):
            fp_sq(k).start()
        for k in far_first:
            fsq_copy(to_peer(k), me).start()

    @pl.when(sec < last)
    def _():
        for c in range(chunks):
            arriving = remote(
                fin.at[core, me, c], fin.at[core, me, c], fp_s, fp_r.at[c], (last, me)
            )
            arriving.wait_recv()
            for k in far_first:
                fin_copy(c, to_peer(k), me).start()

            @pl.when(sec < last - 1)
            def _():
                sib_copy(c, core, me).start()

        arriving = remote(
            fsq_in.at[me], fsq_in.at[me], fq_s, fp_r.at[chunks], (last, me)
        )
        arriving.wait_recv()
        for k in far_first:
            fsq_copy(to_peer(k), me).start()

    hw_copy.wait()

    def whole(piece, slot, send, recv):
        return remote(fin.at[piece, slot], fin.at[piece, slot], send, recv.at[slot], (sibling, me))

    def pass_on(k):
        _, peer = mate(me, k, n)
        whole(core, peer, fin_s, fin_r).wait_recv()
        for c in range(chunks):
            sib_copy(c, core, peer).start()

    def head(k, logits):
        _, peer = mate(me, k, n)
        if isinstance(k, int) and k == 0:

            @pl.when(sec < last)
            def _():
                whole(1 - core, peer, sib_s, sib_r).wait_recv()

        else:
            whole(1 - core, peer, sib_s, sib_r).wait_recv()
        for c in range(chunks):
            at = pl.ds(pl.multiple_of(peer * width + c * chunk, chunk), chunk)
            both = jnp.concatenate([fin[0, peer, c], fin[1, peer, c]], axis=0)
            logits = logits + jnp.dot(both, hw[at, :], preferred_element_type=F32)
        return logits

    lag = min(2, n - 1)
    for k in range(1, lag + 1):
        pass_on(k)
    logits = head(0, jnp.zeros(out.shape, F32))

    def step(k, logits):
        pass_on(k)
        return head(k - lag, logits)

    logits = lax.fori_loop(lag + 1, n, step, logits)
    logits = lax.fori_loop(n - lag, n, head, logits)
    all_fsq = remote(
        fsq_in.at[pl.ds(1, n - 1)], fsq_in.at[pl.ds(1, n - 1)], fsq_s, fsq_r, (sec, me)
    )
    all_fsq.wait_recv()
    squares = jnp.sum(fsq_in[:, 0, :], axis=0, keepdims=True)
    logits = logits * lax.rsqrt(to_col(squares) / (n * width) + EPS)
    vocab = out.shape[1]
    ids = (mine * vocab + lax.broadcasted_iota(jnp.int32, (1, vocab), 1)).astype(F32)
    picked = jnp.sum(jnp.where(ids == target_v[:, 0:1], logits, 0.0), axis=1, keepdims=True)
    top = jnp.max(logits, axis=1, keepdims=True)
    amount = jnp.sum(jnp.exp(logits - top), axis=1, keepdims=True)
    row_of = lax.broadcasted_iota(jnp.int32, (rows, 128), 0)
    lane_of = lax.broadcasted_iota(jnp.int32, (rows, 128), 1)
    packed = jnp.where(lane_of == row_of, top, 0.0)
    packed = jnp.where(lane_of == row_of + rows, amount, packed)
    packed = jnp.where(lane_of == row_of + 2 * rows, picked, packed)
    red[...] = jnp.sum(packed, axis=0, keepdims=True)

    def red_copy(other, slot):
        return remote(
            red, red_in.at[slot], red_s, red_r, (other // n, lax.rem(other, n))
        )

    if total <= 64:
        for k in range(total - 1, 0, -1):
            red_copy(mate(mine, k, total)[0], mine).start()
    else:

        def red_start(k, carry):
            red_copy(mate(mine, total - k, total)[0], mine).start()
            return carry

        lax.fori_loop(1, total, red_start, 0)
    red_in[mine] = red[...]
    flat[...] = logits

    def sent(ref, sem):
        remote(ref, ref, sem, sem, (sec, me)).wait_send()

    others_n = pl.ds(1, n - 1)
    sent(sq_in.at[others_n], sq_s)
    sent(part_in.at[:, others_n], part_s)
    sent(att_in.at[:, others_n], att_s)
    sent(fin.at[0, others_n], fin_s)
    sent(fin.at[0, others_n], sib_s)
    all_fsq.wait_send()

    @pl.when(sec != last - 1)
    def _():
        sent(fin.at[0, 0], sib_s)

    @pl.when(sec < last)
    def _():
        sent(xo, hop_s)

    @pl.when(sec == last)
    def _():
        sent(fin.at[0, pl.ds(1, sections - 1)], fp_s)
        sent(fsq_in.at[pl.ds(1, sections - 1)], fq_s)

    order = (
        jnp.sum(jnp.where(small_eye, slot_v[...].astype(F32), 0.0), axis=1, keepdims=True)
        == lane_of.astype(F32)
    )
    for s in range(rows):
        out[s : s + 1, :] = flat[pl.ds(slot_s[0, s], 1), :]

    everyone = remote(
        red_in.at[pl.ds(1, total - 1)],
        red_in.at[pl.ds(1, total - 1)],
        red_s,
        red_r,
        (sec, me),
    )
    everyone.wait_recv()
    seen = red_in[:, 0, :]
    row_top = jnp.max(seen, axis=0, keepdims=True)
    amounts = pltpu.roll(seen, 128 - rows, 1)
    row_total = jnp.sum(amounts * jnp.exp(jnp.minimum(seen - row_top, 0.0)), axis=0, keepdims=True)
    log_total = row_top + jnp.log(row_total)
    total_col = jnp.sum(jnp.where(order, log_total, 0.0), axis=1, keepdims=True)
    out[...] = out[...] - total_col
    scored = pltpu.roll(jnp.sum(seen, axis=0, keepdims=True), 128 - 2 * rows, 1) - log_total
    chosen[...] = to_row(jnp.sum(jnp.where(order, scored, 0.0), axis=1, keepdims=True))
    everyone.wait_send()


def local(
    hidden_in,
    lengths,
    assign,
    token_ids,
    attn_gain,
    qkv_weight,
    qkv_bias,
    out_weight,
    kv_cache,
    final_gain,
    head_weight,
):
    sections = lax.axis_size("pipe")
    n = lax.axis_size("mp")
    rows, width = hidden_in.shape
    lc = kv_cache.shape[1]
    qkv = qkv_weight.shape[2]
    inner = out_weight.shape[1]
    vocab = head_weight.shape[1]
    heads_all = HEADS + 2 * KV_HEADS
    half = HEAD_DIM // 2
    frequency = np.float32(THETA) ** (
        -np.arange(half).astype(np.float32) * np.float32(2.0) / np.float32(HEAD_DIM)
    )
    freq = jnp.asarray(np.concatenate([frequency, frequency])[None, :], F32)
    group = HEADS // KV_HEADS
    phases = heads_all // group
    span = lc * group
    dma = pltpu.SemaphoreType.DMA
    vm = pl.BlockSpec(memory_space=pltpu.VMEM)
    hbm = pl.BlockSpec(memory_space=pltpu.HBM)
    total = sections * n
    chunks = 2
    logprobs, chosen = pl.pallas_call(
        functools.partial(kernel, sections, n),
        out_shape=(
            jax.ShapeDtypeStruct((rows, vocab), F32),
            jax.ShapeDtypeStruct((1, 128), F32),
        ),
        in_specs=[hbm] * 12,
        out_specs=(vm, vm),
        scratch_shapes=[
            pltpu.VMEM((width, qkv), BF16),
            pltpu.VMEM((inner, width), BF16),
            pltpu.VMEM(kv_cache.shape[1:], BF16),
            pltpu.VMEM(head_weight.shape, BF16),
            pltpu.VMEM((rows, width), BF16),
            pltpu.VMEM((rows, width), BF16),
            pltpu.VMEM((rows, width), BF16),
            pltpu.VMEM((rows * group, HEAD_DIM), F32),
            pltpu.VMEM((phases, n, span, HEAD_DIM), BF16),
            pltpu.VMEM((phases, n, span, HEAD_DIM), BF16),
            pltpu.VMEM((8, 128), F32),
            pltpu.VMEM((n, 8, 128), F32),
            pltpu.VMEM((1, width), BF16),
            pltpu.VMEM((1, qkv), BF16),
            pltpu.VMEM((width // 128, 128), BF16),
            pltpu.VMEM((1, rows), jnp.int32),
            pltpu.VMEM((1, rows), jnp.int32),
            pltpu.VMEM((1, rows), jnp.int32),
            pltpu.VMEM((1, HEAD_DIM), F32),
            pltpu.SMEM((1, rows), jnp.int32),
            pltpu.VMEM((heads_all, HEAD_DIM), F32),
            pltpu.VMEM((lc, HEAD_DIM), F32),
            pltpu.VMEM((lc, HEAD_DIM), F32),
            pltpu.VMEM((lc, HEAD_DIM), F32),
            pltpu.VMEM((rows, 128), F32),
            pltpu.VMEM((lc, 2 * KV_HEADS, HEAD_DIM), F32),
            pltpu.VMEM((KV_HEADS, span, HEAD_DIM), BF16),
            pltpu.VMEM((KV_HEADS, n, span, HEAD_DIM), BF16),
            pltpu.VMEM((rows, width), F32),
            pltpu.VMEM((2, n, chunks, rows // 2, width // chunks), BF16),
            pltpu.VMEM((n, 1, 128), F32),
            pltpu.VMEM((1, 128), F32),
            pltpu.VMEM((total, 1, 128), F32),
            pltpu.VMEM((rows, vocab), F32),
            dma((phases,)),
            dma((3,)),
            dma((9,)),
            dma,
            dma((phases,)),
            dma,
            dma,
            dma,
            dma((KV_HEADS,)),
            dma,
            dma,
            dma,
            dma((n,)),
            dma,
            dma((n,)),
            dma,
            dma,
            dma,
            dma,
            dma((chunks + 1,)),
            dma,
            dma,
        ],
        compiler_params=pltpu.CompilerParams(
            collective_id=0, has_side_effects=True, vmem_limit_bytes=60 * 1024 * 1024
        ),
    )(
        hidden_in,
        lengths.reshape(1, rows),
        assign.reshape(1, rows),
        token_ids.reshape(1, rows),
        attn_gain,
        qkv_weight,
        qkv_bias,
        out_weight,
        kv_cache,
        final_gain.reshape(width // 128, 128),
        head_weight,
        freq,
    )
    return logprobs, chosen[0, :rows]


def solution(mesh):
    return jax.shard_map(
        local,
        mesh=mesh,
        in_specs=(
            P(None, "mp"),
            P(),
            P(),
            P(),
            P("pipe", "mp"),
            P("pipe", "mp", None),
            P("pipe", None),
            P("pipe", None, "mp"),
            P("pipe", "mp", None, None, None, None),
            P("mp"),
            P(None, ("pipe", "mp")),
        ),
        out_specs=(P(None, ("pipe", "mp")), P()),
        check_vma=False,
    )
```

time: 95.3 us -> 85.5 us (0.90)
  Pallas kernels: 90.6 us -> 82.1 us
  local copies, waits for them, and re-layouts: 3.84 us -> 2.57 us
    pallas_call x1, Pallas kernels: 90.6 us -> 82.1 us  [local(): pl.pallas_call(functools.partial(kernel, sections, n), out_shape=(jax.Sha...]
    reshape x1 -> x0, local copies, waits for them, and re-layouts: 1.28 us -> none  [local(): final_gain.reshape(1, width)]
where the time goes in v1:
time: 85.5 us; the launch traced here: 85.4 us
  Pallas kernels  82.1 us (96%)
  local copies, waits for them, and re-layouts  2.57 us (3%)
    pallas_call x1, Pallas kernels, local(): pl.pallas_call(functools.partial(kernel, sections, n), out_shape=(jax.Sha...  82.1 us

profile of v1, /device:TPU:0, one launch (start us, length us, event | category | flops | bytes accessed | tf_op | source)
XLA Modules:
  0.0 85.4 jit_solution(9720679218942558781)
XLA Ops:
  0.6 82.1 %shard_map.131 = (f32[32,384]{1,0:T(8,128)}, f32[1,128]{1,0:T(1,128)}) custom-call(bf16[32,1024]{1,0:T(8,128)(2,1)} %hidden.1, s32[1,32]{1,0:T(1,128)} %bitcast.7, s32[1,32]{1,0:T(1,128)} %bitcast.8, s32[1,32]{1,0:T(1,128)} %bitcast.9, bf16[1,1024]{1,0:T(2,128)(2,1)} %gain.1, bf16[1,1024,5120]{2,1,0:T(8,128)(2,1)} %qkv_weight.1, bf16[1,5120]{1,0:T(2,128)(2,1)} %bias.1, ...), custom_call_target="tpu_custom_call" | custom-call | tf_op jit(solution)/shard_map/pallas_call | solution.py:710
  82.8 1.1 %slice_bitcast_fusion = f32[32]{0:T(128)} fusion(f32[1,128]{1,0:T(1,128)} %get-tuple-element.5), kind=kLoop, calls=%fused_computation | loop fusion | bytes 256 | tf_op jit(solution)/shard_map/squeeze | solution.py:793
  83.9 1.4 %copy.15 = f32[32,384]{1,0:T(8,128)} copy(f32[32,384]{1,0:T(8,128)} %get-tuple-element.8) | data formatting | bytes 98304

commit v2 on v1

--- a/solution.py
+++ b/solution.py
@@ -226,16 +226,25 @@
             jnp.where(small_eye, token_v[...].astype(F32), 0.0), axis=1, keepdims=True
         )
         target_v[...] = jnp.broadcast_to(target, target_v.shape)
+        length = jnp.concatenate(
+            [
+                jnp.sum(
+                    jnp.where(lane_rows == me * lc + i, len_v[...].astype(F32), 0.0),
+                    axis=1,
+                    keepdims=True,
+                )
+                for i in range(lc)
+            ],
+            axis=0,
+        )
+        angles = length * freq_v[...]
+        cosines = jnp.cos(angles)
+        sines = jnp.sin(angles) * jnp.where(lane < HEAD_DIM // 2, -1.0, 1.0)
         for i in range(lc):
-            length = jnp.sum(
-                jnp.where(lane_rows == me * lc + i, len_v[...].astype(F32), 0.0),
-                axis=1,
-                keepdims=True,
-            )
-            own_rows[i : i + 1, :] = jnp.broadcast_to(length, (1, HEAD_DIM))
-        angles = own_rows[...] * freq_v[...]
-        turn_cos[...] = jnp.cos(angles)
-        turn_sin[...] = jnp.sin(angles) * jnp.where(lane < HEAD_DIM // 2, -1.0, 1.0)
+            own = slice(i * group, (i + 1) * group)
+            own_rows[own, :] = jnp.broadcast_to(length[i : i + 1], (group, HEAD_DIM))
+            turn_cos[own, :] = jnp.broadcast_to(cosines[i : i + 1], (group, HEAD_DIM))
+            turn_sin[own, :] = jnp.broadcast_to(sines[i : i + 1], (group, HEAD_DIM))
 
     def scale_rows():
         gain_copy.wait()
@@ -298,7 +307,8 @@
 
     @pl.when(sec == 0)
     def _():
-        hidden_copy.wait()
+        with jax.named_scope("hidden_wait"):
+            hidden_copy.wait()
         scale_rows()
         wq_rest()
         for copy in others:
@@ -309,7 +319,8 @@
     def _():
         set_up()
 
-    pl.semaphore_wait(barrier, n + sections - 2)
+    with jax.named_scope("barrier"):
+        pl.semaphore_wait(barrier, n + sections - 2)
 
     @pl.when(sec == 0)
     def _():
@@ -318,7 +329,8 @@
 
     @pl.when(sec > 0)
     def _():
-        remote(xo, x, hop_s, hop_r, (sec - 1, me)).wait_recv()
+        with jax.named_scope("hop_wait"):
+            remote(xo, x, hop_s, hop_r, (sec - 1, me)).wait_recv()
         scale_rows()
         sq_send()
 
@@ -332,89 +344,89 @@
         set_up()
 
     def summed(phase):
-        remote(
-            part.at[phase, pl.ds(1, n - 1)],
-            part_in.at[phase, pl.ds(1, n - 1)],
-            part_s,
-            part_r.at[phase],
-            (sec, me),
-        ).wait_recv()
+        with jax.named_scope("rs_wait"):
+            remote(
+                part.at[phase, pl.ds(1, n - 1)],
+                part_in.at[phase, pl.ds(1, n - 1)],
+                part_s,
+                part_r.at[phase],
+                (sec, me),
+            ).wait_recv()
         result = part_in[phase, 0].astype(F32)
         for p in range(1, n):
             result = result + part_in[phase, p].astype(F32)
         return result
 
-    remote(
-        sq_in.at[pl.ds(1, n - 1)], sq_in.at[pl.ds(1, n - 1)], sq_s, sq_r, (sec, me)
-    ).wait_recv()
+    with jax.named_scope("sq_wait"):
+        remote(
+            sq_in.at[pl.ds(1, n - 1)], sq_in.at[pl.ds(1, n - 1)], sq_s, sq_r, (sec, me)
+        ).wait_recv()
     squares = sq_in[0]
     for p in range(1, n):
         squares = squares + sq_in[p]
-    factor = [
-        lax.rsqrt(
-            jnp.sum(
-                jnp.where(lane == me * lc + i, squares[0:1, :], 0.0), axis=1, keepdims=True
-            )
-            / (n * width)
-            + EPS
-        )
-        for i in range(lc)
-    ]
-    own_len = [own_rows[i : i + 1, 0:1] for i in range(lc)]
-    cosine = turn_cos[...]
-    sine = turn_sin[...]
-
-    def turn(block, i):
-        return (
-            block * cosine[i : i + 1]
-            + pltpu.roll(block, HEAD_DIM // 2, 1) * sine[i : i + 1]
-        )
-
-    is_key = lax.broadcasted_iota(jnp.int32, (2 * KV_HEADS, HEAD_DIM), 0) < KV_HEADS
-    block_sum = summed(phases - 1)
-    for i in range(lc):
-        block = block_sum[i * group : (i + 1) * group] * factor[i] + bias_rows[HEADS:, :]
-        fresh[i] = jnp.where(is_key, turn(block, i), block).astype(BF16).astype(F32)
+    own_request = me * lc + lax.broadcasted_iota(jnp.int32, (span, 128), 0) // group
+    own_lane = lax.broadcasted_iota(jnp.int32, (span, 128), 1)
+    factor = lax.rsqrt(
+        jnp.sum(jnp.where(own_lane == own_request, squares[0:1, :], 0.0), axis=1, keepdims=True)
+        / (n * width)
+        + EPS
+    )
+    pos = lax.broadcasted_iota(jnp.int32, (1, kv.shape[3]), 1).astype(F32)
+
+    def turned(block):
+        return block * turn_cos[...] + pltpu.roll(block, HEAD_DIM // 2, 1) * turn_sin[...]
+
+    def each(rows_of):
+        return jnp.concatenate([rows_of(i) for i in range(lc)], axis=0)
+
+    def rows_at(i):
+        return slice(i * group, (i + 1) * group)
+
+    is_key = (
+        lax.rem(lax.broadcasted_iota(jnp.int32, (span, HEAD_DIM), 0), 2 * KV_HEADS) < KV_HEADS
+    )
+    fresh_bias = bias_rows[HEADS:, :]
+    block = summed(phases - 1) * factor + each(lambda i: fresh_bias)
+    fresh[...] = jnp.where(is_key, turned(block), block).astype(BF16).astype(F32)
     kv_copy.wait()
-    pos = lax.broadcasted_iota(jnp.int32, (1, kv.shape[3]), 1).astype(F32)
 
     def att_copy(h, peer, slot):
-        return remote(
-            att.at[h], att_in.at[h, slot], att_s, att_r.at[h], (sec, peer)
-        )
+        return remote(att.at[h], att_in.at[h, slot], att_s, att_r.at[h], (sec, peer))
 
     def attend(h, carry):
         block_sum = summed(h)
-        bias_h = bias_rows[pl.ds(pl.multiple_of(h * group, group), group), :]
-        done = []
-        for i in range(lc):
-            block = block_sum[i * group : (i + 1) * group] * factor[i] + bias_h
-            query = turn(block, i).astype(BF16)
-            key_new = fresh[i, pl.ds(h, 1), :]
-            value_new = fresh[i, pl.ds(KV_HEADS + h, 1), :]
-            visible = pos < own_len[i]
-            scores = (
-                lax.dot_general(
-                    query,
+        with jax.named_scope("attend"):
+            bias_h = bias_rows[pl.ds(pl.multiple_of(h * group, group), group), :]
+            query = turned(block_sum * factor + each(lambda i: bias_h))
+            scores = each(
+                lambda i: lax.dot_general(
+                    query[rows_at(i)].astype(BF16),
                     kv[i, 0, h],
                     (((1,), (1,)), ((), ())),
                     preferred_element_type=F32,
                 )
-                * scale
             )
+            scores = scores * scale
+            repeat = lambda row: jnp.broadcast_to(fresh[pl.ds(row, 1), :], (group, HEAD_DIM))
+            key_new = each(lambda i: repeat(i * group + h))
+            value_new = each(lambda i: repeat(i * group + KV_HEADS + h))
             self_score = (
-                jnp.sum(query.astype(F32) * key_new, axis=1, keepdims=True) * scale
+                jnp.sum(query.astype(BF16).astype(F32) * key_new, axis=1, keepdims=True) * scale
             )
+            visible = pos < own_rows[:, 0:1]
             top = jnp.maximum(
                 jnp.max(jnp.where(visible, scores, -1e30), axis=1, keepdims=True), self_score
             )
             weights = jnp.where(visible, jnp.exp(scores - top), 0.0)
             self_weight = jnp.exp(self_score - top)
             denominator = jnp.sum(weights, axis=1, keepdims=True) + self_weight
-            mixed = jnp.dot(weights.astype(BF16), kv[i, 1, h], preferred_element_type=F32)
+            mixed = each(
+                lambda i: jnp.dot(
+                    weights[rows_at(i)].astype(BF16), kv[i, 1, h], preferred_element_type=F32
+                )
+            )
             mixed = mixed + self_weight.astype(BF16).astype(F32) * value_new
-            done.append(mixed / denominator)
-        att[h] = jnp.concatenate(done, axis=0).astype(BF16)
+            att[h] = (mixed / denominator).astype(BF16)
         for k in far_first:
             att_copy(h, to_peer(k), me).start()
         att_in[h, me] = att[h]
@@ -434,7 +446,8 @@
         )
 
     def gathered(h):
-        all_att(h).wait_recv()
+        with jax.named_scope("ag_wait"):
+            all_att(h).wait_recv()
         for p in range(n):
             stage[p * span : (p + 1) * span, :] = att_in[h, p].astype(F32)
         return jnp.concatenate(
@@ -533,7 +546,8 @@
             arriving = remote(
                 fin.at[core, me, c], fin.at[core, me, c], fp_s, fp_r.at[c], (last, me)
             )
-            arriving.wait_recv()
+            with jax.named_scope("fp_wait"):
+                arriving.wait_recv()
             for k in far_first:
                 fin_copy(c, to_peer(k), me).start()
 
@@ -555,7 +569,8 @@
 
     def pass_on(k):
         _, peer = mate(me, k, n)
-        whole(core, peer, fin_s, fin_r).wait_recv()
+        with jax.named_scope("fin_wait"):
+            whole(core, peer, fin_s, fin_r).wait_recv()
         for c in range(chunks):
             sib_copy(c, core, peer).start()
 
@@ -568,7 +583,8 @@
                 whole(1 - core, peer, sib_s, sib_r).wait_recv()
 
         else:
-            whole(1 - core, peer, sib_s, sib_r).wait_recv()
+            with jax.named_scope("sib_wait"):
+                whole(1 - core, peer, sib_s, sib_r).wait_recv()
         for c in range(chunks):
             at = pl.ds(pl.multiple_of(peer * width + c * chunk, chunk), chunk)
             both = jnp.concatenate([fin[0, peer, c], fin[1, peer, c]], axis=0)
@@ -660,7 +676,8 @@
         red_r,
         (sec, me),
     )
-    everyone.wait_recv()
+    with jax.named_scope("red_wait"):
+        everyone.wait_recv()
     seen = red_in[:, 0, :]
     row_top = jnp.max(seen, axis=0, keepdims=True)
     amounts = pltpu.roll(seen, 128 - rows, 1)
@@ -670,7 +687,8 @@
     out[...] = out[...] - total_col
     scored = pltpu.roll(jnp.sum(seen, axis=0, keepdims=True), 128 - 2 * rows, 1) - log_total
     chosen[...] = to_row(jnp.sum(jnp.where(order, scored, 0.0), axis=1, keepdims=True))
-    everyone.wait_send()
+    with jax.named_scope("red_sent"):
+        everyone.wait_send()
 
 
 def local(
@@ -737,11 +755,11 @@
             pltpu.VMEM((1, HEAD_DIM), F32),
             pltpu.SMEM((1, rows), jnp.int32),
             pltpu.VMEM((heads_all, HEAD_DIM), F32),
-            pltpu.VMEM((lc, HEAD_DIM), F32),
-            pltpu.VMEM((lc, HEAD_DIM), F32),
-            pltpu.VMEM((lc, HEAD_DIM), F32),
+            pltpu.VMEM((span, HEAD_DIM), F32),
+            pltpu.VMEM((span, HEAD_DIM), F32),
+            pltpu.VMEM((span, HEAD_DIM), F32),
             pltpu.VMEM((rows, 128), F32),
-            pltpu.VMEM((lc, 2 * KV_HEADS, HEAD_DIM), F32),
+            pltpu.VMEM((span, HEAD_DIM), F32),
             pltpu.VMEM((KV_HEADS, span, HEAD_DIM), BF16),
             pltpu.VMEM((KV_HEADS, n, span, HEAD_DIM), BF16),
             pltpu.VMEM((rows, width), F32),

time: 85.5 us -> 78.8 us (0.922)
  Pallas kernels: 82.1 us -> 75.4 us
    pallas_call x1, Pallas kernels: 82.1 us -> 75.4 us  [local(): pl.pallas_call(functools.partial(kernel, sections, n), out_shape=(jax.Sha...]
where the time goes in v2:
time: 78.8 us; the launch traced here: 78.6 us
  Pallas kernels  75.4 us (96%)
  local copies, waits for them, and re-layouts  2.57 us (3%)
    pallas_call x1, Pallas kernels, local(): pl.pallas_call(functools.partial(kernel, sections, n), out_shape=(jax.Sha...  75.4 us

profile of v2, /device:TPU:0, one launch (start us, length us, event | category | flops | bytes accessed | tf_op | source)
XLA Modules:
  0.0 78.6 jit_solution(13259962059437993031)
XLA Ops:
  0.6 75.4 %shard_map.131 = (f32[32,384]{1,0:T(8,128)}, f32[1,128]{1,0:T(1,128)}) custom-call(bf16[32,1024]{1,0:T(8,128)(2,1)} %hidden.1, s32[1,32]{1,0:T(1,128)} %bitcast.7, s32[1,32]{1,0:T(1,128)} %bitcast.8, s32[1,32]{1,0:T(1,128)} %bitcast.9, bf16[1,1024]{1,0:T(2,128)(2,1)} %gain.1, bf16[1,1024,5120]{2,1,0:T(8,128)(2,1)} %qkv_weight.1, bf16[1,5120]{1,0:T(2,128)(2,1)} %bias.1, ...), custom_call_target="tpu_custom_call" | custom-call | tf_op jit(solution)/shard_map/pallas_call | solution.py:728
  76.0 1.1 %slice_bitcast_fusion = f32[32]{0:T(128)} fusion(f32[1,128]{1,0:T(1,128)} %get-tuple-element.5), kind=kLoop, calls=%fused_computation | loop fusion | bytes 256 | tf_op jit(solution)/shard_map/squeeze | solution.py:811
  77.2 1.4 %copy.15 = f32[32,384]{1,0:T(8,128)} copy(f32[32,384]{1,0:T(8,128)} %get-tuple-element.8) | data formatting | bytes 98304

commit v3 on v2

--- a/solution.py
+++ b/solution.py
@@ -102,12 +102,14 @@
     fp_r,
     red_s,
     red_r,
+    help_s,
+    help_r,
 ):
     sec = lax.axis_index("pipe")
     me = lax.axis_index("mp")
     total = sections * n
     rows, width = x.shape
-    lc = kv.shape[0]
+    lc = kv.shape[1]
     heads_all = HEADS + 2 * KV_HEADS
     group = HEADS // KV_HEADS
     phases = heads_all // group
@@ -121,6 +123,10 @@
     core = lax.rem(sec, 2)
     sibling = sec + 1 - 2 * core
     mine = sec * n + me
+    runs = (sec < 2) | (core == 1)
+    helps = (sec >= 2) & (core == 0)
+    helped = (sec >= 2) & (core == 1)
+    following = jnp.where(sec == 0, 1, sec + 2)
     early = min(2, phases)
 
     def mate(own, k, count):
@@ -149,7 +155,7 @@
 
     def wq_copy(c):
         cols = pl.ds(pl.multiple_of(c * cw, cw), cw)
-        return pltpu.make_async_copy(qkv_weight.at[0, :, cols], wq.at[:, cols], wq_sem.at[c])
+        return pltpu.make_async_copy(qkv_weight.at[0, :, cols], wq.at[1, :, cols], wq_sem.at[c])
 
     def phase_of(k):
         return lax.rem(k + phases - 1, phases)
@@ -158,9 +164,9 @@
         return pltpu.make_async_copy(src, dst, small_sem.at[i])
 
     hidden_copy = small(0, hidden, x)
-    gain_copy = small(1, gain, gain_v)
+    gain_copy = small(1, gain, gain_v.at[1])
     others = [
-        small(2, bias, bias_v),
+        small(2, bias, bias_v.at[1]),
         small(3, final_gain, final_v),
         small(4, lengths, len_v),
         small(5, assign, slot_v),
@@ -173,16 +179,18 @@
     def _():
         hidden_copy.start()
 
-    gain_copy.start()
-    for k in range(early):
-        wq_copy((k + phases - 1) % phases).start()
+    @pl.when(runs)
+    def _():
+        gain_copy.start()
+        for k in range(early):
+            wq_copy((k + phases - 1) % phases).start()
 
     def wq_rest():
         for k in range(early, phases):
             wq_copy((k + phases - 1) % phases).start()
 
-    kv_copy = pltpu.make_async_copy(cache.at[0], kv, w_sem.at[0])
-    wo_copy = pltpu.make_async_copy(out_weight.at[0], wo, w_sem.at[1])
+    kv_copy = pltpu.make_async_copy(cache.at[0], kv.at[1], w_sem.at[0])
+    wo_copy = pltpu.make_async_copy(out_weight.at[0], wo.at[1], w_sem.at[1])
     hw_copy = pltpu.make_async_copy(head_weight, hw, w_sem.at[2])
 
     barrier = pltpu.get_barrier_semaphore()
@@ -196,10 +204,24 @@
     def _():
         for copy in others:
             copy.start()
+        hw_copy.start()
+
+    @pl.when((sec > 0) & runs)
+    def _():
         wq_rest()
         kv_copy.start()
         wo_copy.start()
-        hw_copy.start()
+
+    def help_copy(i, src, dst):
+        return remote(src, dst, help_s, help_r.at[i], (sibling, me))
+
+    help_copies = [
+        help_copy(0, gain, gain_v.at[0]),
+        help_copy(1, bias, bias_v.at[0]),
+        help_copy(2, qkv_weight.at[0], wq.at[0]),
+        help_copy(3, cache.at[0], kv.at[0]),
+        help_copy(4, out_weight.at[0], wo.at[0]),
+    ]
 
     eye = lax.broadcasted_iota(jnp.int32, (rows, 128), 0) == lax.broadcasted_iota(
         jnp.int32, (rows, 128), 1
@@ -217,11 +239,16 @@
         jnp.int32, (rows, rows), 1
     )
 
+    def set_bias(t):
+        for i in range(heads_all):
+            bias_rows[t, i : i + 1, :] = bias_v[
+                t, :, i * HEAD_DIM : (i + 1) * HEAD_DIM
+            ].astype(F32)
+
     def set_up():
         for copy in others:
             copy.wait()
-        for i in range(heads_all):
-            bias_rows[i : i + 1, :] = bias_v[:, i * HEAD_DIM : (i + 1) * HEAD_DIM].astype(F32)
+        set_bias(1)
         target = jnp.sum(
             jnp.where(small_eye, token_v[...].astype(F32), 0.0), axis=1, keepdims=True
         )
@@ -246,59 +273,62 @@
             turn_cos[own, :] = jnp.broadcast_to(cosines[i : i + 1], (group, HEAD_DIM))
             turn_sin[own, :] = jnp.broadcast_to(sines[i : i + 1], (group, HEAD_DIM))
 
-    def scale_rows():
-        gain_copy.wait()
+    def scale_rows(t):
         current = x[...].astype(F32)
-        sq[...] = jnp.broadcast_to(
-            to_row(jnp.sum(current * current, axis=1, keepdims=True)), sq.shape
-        )
-        scaled[...] = (current * gain_v[...].astype(F32)).astype(BF16)
-
-    def sq_copy(peer, slot):
-        return remote(sq, sq_in.at[slot], sq_s, sq_r, (sec, peer))
-
-    def sq_send():
+        sq[t] = jnp.broadcast_to(
+            to_row(jnp.sum(current * current, axis=1, keepdims=True)), sq.shape[1:]
+        )
+        scaled[...] = (current * gain_v[t].astype(F32)).astype(BF16)
+
+    def sq_copy(t, peer, slot):
+        return remote(sq.at[t], sq_in.at[t, slot], sq_s.at[t], sq_r.at[t], (sec, peer))
+
+    def sq_send(t):
         for k in far_first:
-            sq_copy(to_peer(k), me).start()
-        sq_in[me] = sq[...]
-
-    def part_copy(phase, peer, slot):
+            sq_copy(t, to_peer(k), me).start()
+        sq_in[t, me] = sq[t]
+
+    def part_copy(t, phase, peer, slot):
         return remote(
-            part.at[phase, peer],
-            part_in.at[phase, slot],
-            part_s,
-            part_r.at[phase],
+            part.at[t, phase, peer],
+            part_in.at[t, phase, slot],
+            part_s.at[t],
+            part_r.at[t, phase],
             (sec, peer),
         )
 
-    def multiply(phase):
-        wq_copy(phase).wait()
+    def multiply(t, phase):
+        if t == 1:
+            wq_copy(phase).wait()
         base = pl.multiple_of(phase * cw, cw)
-        piece = jnp.dot(scaled[...], wq[:, pl.ds(base, cw)], preferred_element_type=F32)
+        piece = jnp.dot(scaled[...], wq[t, :, pl.ds(base, cw)], preferred_element_type=F32)
         for j in range(group):
             stage[pl.ds(j, rows, stride=group), :] = piece[
                 :, j * HEAD_DIM : (j + 1) * HEAD_DIM
             ]
         for p in range(n):
-            part[phase, p] = stage[p * span : (p + 1) * span, :].astype(BF16)
-
-    def spread(phase):
+            part[t, phase, p] = stage[p * span : (p + 1) * span, :].astype(BF16)
+
+    def spread(t, phase):
         for k in far_first:
-            part_copy(phase, to_peer(k), me).start()
-        part_in[phase, me] = part[phase, me]
+            part_copy(t, phase, to_peer(k), me).start()
+        part_in[t, phase, me] = part[t, phase, me]
 
     def compute_only(k, carry):
-        multiply(phase_of(k))
+        multiply(1, phase_of(k))
         return carry
 
     def send_only(k, carry):
-        spread(phase_of(k))
+        spread(1, phase_of(k))
         return carry
 
-    def project(k, carry):
-        multiply(phase_of(k))
-        spread(phase_of(k))
-        return carry
+    def project(t):
+        def one(k, carry):
+            multiply(t, phase_of(k))
+            spread(t, phase_of(k))
+            return carry
+
+        return one
 
     def hop_copy(c, to):
         cols = pl.ds(c * chunk, chunk)
@@ -309,7 +339,8 @@
     def _():
         with jax.named_scope("hidden_wait"):
             hidden_copy.wait()
-        scale_rows()
+        gain_copy.wait()
+        scale_rows(1)
         wq_rest()
         for copy in others:
             copy.start()
@@ -322,19 +353,193 @@
     with jax.named_scope("barrier"):
         pl.semaphore_wait(barrier, n + sections - 2)
 
+    @pl.when(helps)
+    def _():
+        for copy in help_copies:
+            copy.start()
+
+    pos = lax.broadcasted_iota(jnp.int32, (1, kv.shape[4]), 1).astype(F32)
+    own_request = me * lc + lax.broadcasted_iota(jnp.int32, (span, 128), 0) // group
+    own_lane = lax.broadcasted_iota(jnp.int32, (span, 128), 1)
+    is_key = (
+        lax.rem(lax.broadcasted_iota(jnp.int32, (span, HEAD_DIM), 0), 2 * KV_HEADS) < KV_HEADS
+    )
+
+    def turned(block):
+        return block * turn_cos[...] + pltpu.roll(block, HEAD_DIM // 2, 1) * turn_sin[...]
+
+    def each(rows_of):
+        return jnp.concatenate([rows_of(i) for i in range(lc)], axis=0)
+
+    def rows_at(i):
+        return slice(i * group, (i + 1) * group)
+
+    def att_copy(t, h, peer, slot):
+        return remote(
+            att.at[t, h], att_in.at[t, h, slot], att_s.at[t], att_r.at[t, h], (sec, peer)
+        )
+
+    def all_att(t, h):
+        return remote(
+            att_in.at[t, h, pl.ds(1, n - 1)],
+            att_in.at[t, h, pl.ds(1, n - 1)],
+            att_s.at[t],
+            att_r.at[t, h],
+            (sec, me),
+        )
+
+    def summed(t, phase):
+        with jax.named_scope("rs_wait"):
+            remote(
+                part.at[t, phase, pl.ds(1, n - 1)],
+                part_in.at[t, phase, pl.ds(1, n - 1)],
+                part_s.at[t],
+                part_r.at[t, phase],
+                (sec, me),
+            ).wait_recv()
+        result = part_in[t, phase, 0].astype(F32)
+        for p in range(1, n):
+            result = result + part_in[t, phase, p].astype(F32)
+        return result
+
+    def attention(t):
+        with jax.named_scope("sq_wait"):
+            remote(
+                sq_in.at[t, pl.ds(1, n - 1)],
+                sq_in.at[t, pl.ds(1, n - 1)],
+                sq_s.at[t],
+                sq_r.at[t],
+                (sec, me),
+            ).wait_recv()
+        squares = sq_in[t, 0]
+        for p in range(1, n):
+            squares = squares + sq_in[t, p]
+        factor = lax.rsqrt(
+            jnp.sum(
+                jnp.where(own_lane == own_request, squares[0:1, :], 0.0), axis=1, keepdims=True
+            )
+            / (n * width)
+            + EPS
+        )
+        fresh_bias = bias_rows[t, HEADS:, :]
+        block = summed(t, phases - 1) * factor + each(lambda i: fresh_bias)
+        fresh[...] = jnp.where(is_key, turned(block), block).astype(BF16).astype(F32)
+        if t == 1:
+            kv_copy.wait()
+        else:
+            help_copies[3].wait_recv()
+
+        def attend(h, carry):
+            block_sum = summed(t, h)
+            with jax.named_scope("attend"):
+                bias_h = bias_rows[t, pl.ds(pl.multiple_of(h * group, group), group), :]
+                query = turned(block_sum * factor + each(lambda i: bias_h))
+                scores = each(
+                    lambda i: lax.dot_general(
+                        query[rows_at(i)].astype(BF16),
+                        kv[t, i, 0, h],
+                        (((1,), (1,)), ((), ())),
+                        preferred_element_type=F32,
+                    )
+                )
+                scores = scores * scale
+                repeat = lambda row: jnp.broadcast_to(
+                    fresh[pl.ds(row, 1), :], (group, HEAD_DIM)
+                )
+                key_new = each(lambda i: repeat(i * group + h))
+                value_new = each(lambda i: repeat(i * group + KV_HEADS + h))
+                self_score = (
+                    jnp.sum(query.astype(BF16).astype(F32) * key_new, axis=1, keepdims=True)
+                    * scale
+                )
+                visible = pos < own_rows[:, 0:1]
+                top = jnp.maximum(
+                    jnp.max(jnp.where(visible, scores, -1e30), axis=1, keepdims=True),
+                    self_score,
+                )
+                weights = jnp.where(visible, jnp.exp(scores - top), 0.0)
+                self_weight = jnp.exp(self_score - top)
+                denominator = jnp.sum(weights, axis=1, keepdims=True) + self_weight
+                mixed = each(
+                    lambda i: jnp.dot(
+                        weights[rows_at(i)].astype(BF16),
+                        kv[t, i, 1, h],
+                        preferred_element_type=F32,
+                    )
+                )
+                mixed = mixed + self_weight.astype(BF16).astype(F32) * value_new
+                att[t, h] = (mixed / denominator).astype(BF16)
+            for k in far_first:
+                att_copy(t, h, to_peer(k), me).start()
+            att_in[t, h, me] = att[t, h]
+            return carry
+
+        lax.fori_loop(0, KV_HEADS, attend, 0)
+        if t == 1:
+            wo_copy.wait()
+        else:
+            help_copies[4].wait_recv()
+        update[...] = x[...].astype(F32)
+
+        def project_out(h, carry):
+            mat = gathered(t, h)
+            depth = pl.ds(pl.multiple_of(h * cw, cw), cw)
+            update[...] += jnp.dot(mat, wo[t, depth, :], preferred_element_type=F32)
+            return carry
+
+        lax.fori_loop(0, KV_HEADS - 1, project_out, 0)
+
+    def gathered(t, h):
+        with jax.named_scope("ag_wait"):
+            all_att(t, h).wait_recv()
+        for p in range(n):
+            stage[p * span : (p + 1) * span, :] = att_in[t, h, p].astype(F32)
+        return jnp.concatenate(
+            [stage[pl.ds(j, rows, stride=group), :].astype(BF16) for j in range(group)],
+            axis=1,
+        )
+
+    top_rows = (KV_HEADS - 1) * cw
+
+    def grown(t, mat, cols):
+        return (
+            update[:, cols]
+            + jnp.dot(
+                mat, wo[t, top_rows : top_rows + cw, cols], preferred_element_type=F32
+            )
+        ).astype(BF16)
+
     @pl.when(sec == 0)
     def _():
-        sq_send()
+        sq_send(1)
         lax.fori_loop(0, early, send_only, 0)
 
-    @pl.when(sec > 0)
-    def _():
+    @pl.when(core == 1)
+    def _():
+        gain_copy.wait()
         with jax.named_scope("hop_wait"):
             remote(xo, x, hop_s, hop_r, (sec - 1, me)).wait_recv()
-        scale_rows()
-        sq_send()
-
-    lax.fori_loop(jnp.where(sec == 0, early, 0), phases, project, 0)
+
+    @pl.when(helped)
+    def _():
+        help_copies[0].wait_recv()
+        help_copies[1].wait_recv()
+        help_copies[2].wait_recv()
+        scale_rows(0)
+        sq_send(0)
+        lax.fori_loop(0, phases, project(0), 0)
+        set_bias(0)
+        attention(0)
+        x[...] = grown(0, gathered(0, KV_HEADS - 1), slice(0, width))
+
+    @pl.when(core == 1)
+    def _():
+        scale_rows(1)
+        sq_send(1)
+
+    @pl.when(runs)
+    def _():
+        lax.fori_loop(jnp.where(sec == 0, early, 0), phases, project(1), 0)
 
     @pl.when(sec == 0)
     def _():
@@ -342,126 +547,6 @@
         wo_copy.start()
         hw_copy.start()
         set_up()
-
-    def summed(phase):
-        with jax.named_scope("rs_wait"):
-            remote(
-                part.at[phase, pl.ds(1, n - 1)],
-                part_in.at[phase, pl.ds(1, n - 1)],
-                part_s,
-                part_r.at[phase],
-                (sec, me),
-            ).wait_recv()
-        result = part_in[phase, 0].astype(F32)
-        for p in range(1, n):
-            result = result + part_in[phase, p].astype(F32)
-        return result
-
-    with jax.named_scope("sq_wait"):
-        remote(
-            sq_in.at[pl.ds(1, n - 1)], sq_in.at[pl.ds(1, n - 1)], sq_s, sq_r, (sec, me)
-        ).wait_recv()
-    squares = sq_in[0]
-    for p in range(1, n):
-        squares = squares + sq_in[p]
-    own_request = me * lc + lax.broadcasted_iota(jnp.int32, (span, 128), 0) // group
-    own_lane = lax.broadcasted_iota(jnp.int32, (span, 128), 1)
-    factor = lax.rsqrt(
-        jnp.sum(jnp.where(own_lane == own_request, squares[0:1, :], 0.0), axis=1, keepdims=True)
-        / (n * width)
-        + EPS
-    )
-    pos = lax.broadcasted_iota(jnp.int32, (1, kv.shape[3]), 1).astype(F32)
-
-    def turned(block):
-        return block * turn_cos[...] + pltpu.roll(block, HEAD_DIM // 2, 1) * turn_sin[...]
-
-    def each(rows_of):
-        return jnp.concatenate([rows_of(i) for i in range(lc)], axis=0)
-
-    def rows_at(i):
-        return slice(i * group, (i + 1) * group)
-
-    is_key = (
-        lax.rem(lax.broadcasted_iota(jnp.int32, (span, HEAD_DIM), 0), 2 * KV_HEADS) < KV_HEADS
-    )
-    fresh_bias = bias_rows[HEADS:, :]
-    block = summed(phases - 1) * factor + each(lambda i: fresh_bias)
-    fresh[...] = jnp.where(is_key, turned(block), block).astype(BF16).astype(F32)
-    kv_copy.wait()
-
-    def att_copy(h, peer, slot):
-        return remote(att.at[h], att_in.at[h, slot], att_s, att_r.at[h], (sec, peer))
-
-    def attend(h, carry):
-        block_sum = summed(h)
-        with jax.named_scope("attend"):
-            bias_h = bias_rows[pl.ds(pl.multiple_of(h * group, group), group), :]
-            query = turned(block_sum * factor + each(lambda i: bias_h))
-            scores = each(
-                lambda i: lax.dot_general(
-                    query[rows_at(i)].astype(BF16),
-                    kv[i, 0, h],
-                    (((1,), (1,)), ((), ())),
-                    preferred_element_type=F32,
-                )
-            )
-            scores = scores * scale
-            repeat = lambda row: jnp.broadcast_to(fresh[pl.ds(row, 1), :], (group, HEAD_DIM))
-            key_new = each(lambda i: repeat(i * group + h))
-            value_new = each(lambda i: repeat(i * group + KV_HEADS + h))
-            self_score = (
-                jnp.sum(query.astype(BF16).astype(F32) * key_new, axis=1, keepdims=True) * scale
-            )
-            visible = pos < own_rows[:, 0:1]
-            top = jnp.maximum(
-                jnp.max(jnp.where(visible, scores, -1e30), axis=1, keepdims=True), self_score
-            )
-            weights = jnp.where(visible, jnp.exp(scores - top), 0.0)
-            self_weight = jnp.exp(self_score - top)
-            denominator = jnp.sum(weights, axis=1, keepdims=True) + self_weight
-            mixed = each(
-                lambda i: jnp.dot(
-                    weights[rows_at(i)].astype(BF16), kv[i, 1, h], preferred_element_type=F32
-                )
-            )
-            mixed = mixed + self_weight.astype(BF16).astype(F32) * value_new
-            att[h] = (mixed / denominator).astype(BF16)
-        for k in far_first:
-            att_copy(h, to_peer(k), me).start()
-        att_in[h, me] = att[h]
-        return carry
-
-    lax.fori_loop(0, KV_HEADS, attend, 0)
-    wo_copy.wait()
-    update[...] = x[...].astype(F32)
-
-    def all_att(h):
-        return remote(
-            att_in.at[h, pl.ds(1, n - 1)],
-            att_in.at[h, pl.ds(1, n - 1)],
-            att_s,
-            att_r.at[h],
-            (sec, me),
-        )
-
-    def gathered(h):
-        with jax.named_scope("ag_wait"):
-            all_att(h).wait_recv()
-        for p in range(n):
-            stage[p * span : (p + 1) * span, :] = att_in[h, p].astype(F32)
-        return jnp.concatenate(
-            [stage[pl.ds(j, rows, stride=group), :].astype(BF16) for j in range(group)],
-            axis=1,
-        )
-
-    def project_out(h, carry):
-        mat = gathered(h)
-        depth = pl.ds(pl.multiple_of(h * cw, cw), cw)
-        update[...] += jnp.dot(mat, wo[depth, :], preferred_element_type=F32)
-        return carry
-
-    lax.fori_loop(0, KV_HEADS - 1, project_out, 0)
 
     def fin_copy(c, peer, slot):
         return remote(
@@ -499,46 +584,48 @@
             fsq_in.at[me], fsq_in.at[me], fq_s, fp_r.at[chunks], (to, me)
         )
 
-    mat = gathered(KV_HEADS - 1)
-    top_rows = (KV_HEADS - 1) * cw
-    final_sq = jnp.zeros((rows, 1), F32)
-    for c in range(chunks):
-        cols = slice(c * chunk, (c + 1) * chunk)
-        grown = update[:, cols] + jnp.dot(
-            mat, wo[top_rows : top_rows + cw, cols], preferred_element_type=F32
-        )
-        new = grown.astype(BF16)
-        xo[:, cols] = new
-        final = new.astype(F32)
-        final_sq = final_sq + jnp.sum(final * final, axis=1, keepdims=True)
-
-        @pl.when(sec < last)
-        def _():
-            hop_copy(c, sec + 1).start()
+    @pl.when(runs)
+    def _():
+        attention(1)
+        mat = gathered(1, KV_HEADS - 1)
+        final_sq = jnp.zeros((rows, 1), F32)
+        for c in range(chunks):
+            cols = slice(c * chunk, (c + 1) * chunk)
+            new = grown(1, mat, cols)
+            xo[:, cols] = new
+            final = new.astype(F32)
+            final_sq = final_sq + jnp.sum(final * final, axis=1, keepdims=True)
+
+            @pl.when(sec < last)
+            def _():
+                hop_copy(c, following).start()
+
+            @pl.when(sec == last)
+            def _():
+                lanes = chunk // 128
+                row = jnp.concatenate(
+                    [
+                        final_v[c * lanes + i : c * lanes + i + 1, :].astype(F32)
+                        for i in range(lanes)
+                    ],
+                    axis=1,
+                )
+                both = (final * row).astype(BF16)
+                fin[0, me, c] = both[:half]
+                fin[1, me, c] = both[half:]
+                for k in range(1, sections):
+                    fp_copy(c, k).start()
+                for k in far_first:
+                    fin_copy(c, to_peer(k), me).start()
+                sib_copy(c, core, me).start()
 
         @pl.when(sec == last)
         def _():
-            lanes = chunk // 128
-            row = jnp.concatenate(
-                [final_v[c * lanes + i : c * lanes + i + 1, :].astype(F32) for i in range(lanes)],
-                axis=1,
-            )
-            both = (final * row).astype(BF16)
-            fin[0, me, c] = both[:half]
-            fin[1, me, c] = both[half:]
+            fsq_in[me] = to_row(final_sq)
             for k in range(1, sections):
-                fp_copy(c, k).start()
+                fp_sq(k).start()
             for k in far_first:
-                fin_copy(c, to_peer(k), me).start()
-            sib_copy(c, core, me).start()
-
-    @pl.when(sec == last)
-    def _():
-        fsq_in[me] = to_row(final_sq)
-        for k in range(1, sections):
-            fp_sq(k).start()
-        for k in far_first:
-            fsq_copy(to_peer(k), me).start()
+                fsq_copy(to_peer(k), me).start()
 
     @pl.when(sec < last)
     def _():
@@ -642,9 +729,25 @@
         remote(ref, ref, sem, sem, (sec, me)).wait_send()
 
     others_n = pl.ds(1, n - 1)
-    sent(sq_in.at[others_n], sq_s)
-    sent(part_in.at[:, others_n], part_s)
-    sent(att_in.at[:, others_n], att_s)
+
+    def stage_sent(t):
+        sent(sq_in.at[t, others_n], sq_s.at[t])
+        sent(part_in.at[t, :, others_n], part_s.at[t])
+        sent(att_in.at[t, :, others_n], att_s.at[t])
+
+    @pl.when(helped)
+    def _():
+        stage_sent(0)
+
+    @pl.when(runs)
+    def _():
+        stage_sent(1)
+
+    @pl.when(helps)
+    def _():
+        for copy in help_copies:
+            copy.wait_send()
+
     sent(fin.at[0, others_n], fin_s)
     sent(fin.at[0, others_n], sib_s)
     all_fsq.wait_send()
@@ -653,7 +756,7 @@
     def _():
         sent(fin.at[0, 0], sib_s)
 
-    @pl.when(sec < last)
+    @pl.when((sec < last) & runs)
     def _():
         sent(xo, hop_s)
 
@@ -734,34 +837,34 @@
         in_specs=[hbm] * 12,
         out_specs=(vm, vm),
         scratch_shapes=[
-            pltpu.VMEM((width, qkv), BF16),
-            pltpu.VMEM((inner, width), BF16),
-            pltpu.VMEM(kv_cache.shape[1:], BF16),
+            pltpu.VMEM((2, width, qkv), BF16),
+            pltpu.VMEM((2, inner, width), BF16),
+            pltpu.VMEM((2,) + kv_cache.shape[1:], BF16),
             pltpu.VMEM(head_weight.shape, BF16),
             pltpu.VMEM((rows, width), BF16),
             pltpu.VMEM((rows, width), BF16),
             pltpu.VMEM((rows, width), BF16),
             pltpu.VMEM((rows * group, HEAD_DIM), F32),
-            pltpu.VMEM((phases, n, span, HEAD_DIM), BF16),
-            pltpu.VMEM((phases, n, span, HEAD_DIM), BF16),
-            pltpu.VMEM((8, 128), F32),
-            pltpu.VMEM((n, 8, 128), F32),
-            pltpu.VMEM((1, width), BF16),
-            pltpu.VMEM((1, qkv), BF16),
+            pltpu.VMEM((2, phases, n, span, HEAD_DIM), BF16),
+            pltpu.VMEM((2, phases, n, span, HEAD_DIM), BF16),
+            pltpu.VMEM((2, 8, 128), F32),
+            pltpu.VMEM((2, n, 8, 128), F32),
+            pltpu.VMEM((2, 1, width), BF16),
+            pltpu.VMEM((2, 1, qkv), BF16),
             pltpu.VMEM((width // 128, 128), BF16),
             pltpu.VMEM((1, rows), jnp.int32),
             pltpu.VMEM((1, rows), jnp.int32),
             pltpu.VMEM((1, rows), jnp.int32),
             pltpu.VMEM((1, HEAD_DIM), F32),
             pltpu.SMEM((1, rows), jnp.int32),
-            pltpu.VMEM((heads_all, HEAD_DIM), F32),
+            pltpu.VMEM((2, heads_all, HEAD_DIM), F32),
             pltpu.VMEM((span, HEAD_DIM), F32),
             pltpu.VMEM((span, HEAD_DIM), F32),
             pltpu.VMEM((span, HEAD_DIM), F32),
             pltpu.VMEM((rows, 128), F32),
             pltpu.VMEM((span, HEAD_DIM), F32),
-            pltpu.VMEM((KV_HEADS, span, HEAD_DIM), BF16),
-            pltpu.VMEM((KV_HEADS, n, span, HEAD_DIM), BF16),
+            pltpu.VMEM((2, KV_HEADS, span, HEAD_DIM), BF16),
+            pltpu.VMEM((2, KV_HEADS, n, span, HEAD_DIM), BF16),
             pltpu.VMEM((rows, width), F32),
             pltpu.VMEM((2, n, chunks, rows // 2, width // chunks), BF16),
             pltpu.VMEM((n, 1, 128), F32),
@@ -771,12 +874,12 @@
             dma((phases,)),
             dma((3,)),
             dma((9,)),
-            dma,
-            dma((phases,)),
-            dma,
-            dma,
-            dma,
-            dma((KV_HEADS,)),
+            dma((2,)),
+            dma((2, phases)),
+            dma((2,)),
+            dma((2,)),
+            dma((2,)),
+            dma((2, KV_HEADS)),
             dma,
             dma,
             dma,
@@ -790,6 +893,8 @@
             dma((chunks + 1,)),
             dma,
             dma,
+            dma,
+            dma((5,)),
         ],
         compiler_params=pltpu.CompilerParams(
             collective_id=0, has_side_effects=True, vmem_limit_bytes=60 * 1024 * 1024

time: 78.8 us -> 75.4 us (0.957)
  Pallas kernels: 75.4 us -> 72 us
    pallas_call x1, Pallas kernels: 75.4 us -> 72 us  [local(): pl.pallas_call(functools.partial(kernel, sections, n), out_shape=(jax.Sha...]
where the time goes in v3:
time: 75.4 us; the launch traced here: 75.2 us
  Pallas kernels  72 us (95%)
  local copies, waits for them, and re-layouts  2.57 us (3%)
    pallas_call x1, Pallas kernels, local(): pl.pallas_call(functools.partial(kernel, sections, n), out_shape=(jax.Sha...  72 us

profile of v3, /device:TPU:0, one launch (start us, length us, event | category | flops | bytes accessed | tf_op | source)
XLA Modules:
  0.0 75.2 jit_solution(6490669324252299228)
XLA Ops:
  0.6 72.0 %shard_map.131 = (f32[32,384]{1,0:T(8,128)}, f32[1,128]{1,0:T(1,128)}) custom-call(bf16[32,1024]{1,0:T(8,128)(2,1)} %hidden.1, s32[1,32]{1,0:T(1,128)} %bitcast.7, s32[1,32]{1,0:T(1,128)} %bitcast.8, s32[1,32]{1,0:T(1,128)} %bitcast.9, bf16[1,1024]{1,0:T(2,128)(2,1)} %gain.1, bf16[1,1024,5120]{2,1,0:T(8,128)(2,1)} %qkv_weight.1, bf16[1,5120]{1,0:T(2,128)(2,1)} %bias.1, ...), custom_call_target="tpu_custom_call" | custom-call | tf_op jit(solution)/shard_map/pallas_call | solution.py:831
  72.7 1.1 %slice_bitcast_fusion = f32[32]{0:T(128)} fusion(f32[1,128]{1,0:T(1,128)} %get-tuple-element.5), kind=kLoop, calls=%fused_computation | loop fusion | bytes 256 | tf_op jit(solution)/shard_map/squeeze | solution.py:916
  73.8 1.4 %copy.15 = f32[32,384]{1,0:T(8,128)} copy(f32[32,384]{1,0:T(8,128)} %get-tuple-element.8) | data formatting | bytes 98304

commit v4 on v3

--- a/solution.py
+++ b/solution.py
@@ -104,6 +104,7 @@
     red_r,
     help_s,
     help_r,
+    side_s,
 ):
     sec = lax.axis_index("pipe")
     me = lax.axis_index("mp")
@@ -120,6 +121,8 @@
     half = rows // 2
     chunks = fin.shape[2]
     chunk = width // chunks
+    parts = 2
+    cut = width // parts
     core = lax.rem(sec, 2)
     sibling = sec + 1 - 2 * core
     mine = sec * n + me
@@ -331,7 +334,7 @@
         return one
 
     def hop_copy(c, to):
-        cols = pl.ds(c * chunk, chunk)
+        cols = pl.ds(c * cut, cut)
         return remote(xo.at[:, cols], x.at[:, cols], hop_s, hop_r, (to, me))
 
 
@@ -571,6 +574,27 @@
             fsq_in.at[slot], fsq_in.at[slot], fsq_s, fsq_r, (sec, peer)
         )
 
+    across = max(d for d in range(1, n + 1) if n % d == 0 and d * d <= n)
+    relayed = across == 2 and n == 8
+    place = me // across
+    outer = (place == 0) | (place == n // across - 1)
+
+    def fin_send():
+        for k in (1, 6, 4, 5, 7, 2, 3) if relayed else range(1, n):
+            if relayed and k in (5, 7):
+
+                @pl.when(jnp.logical_not(outer))
+                def _():
+                    fin_copy(0, to_peer(k), me).start()
+
+            else:
+                fin_copy(0, to_peer(k), me).start()
+
+    def side_copy(slot):
+        return remote(
+            fin.at[core, slot], fin.at[core, slot], side_s, fin_r.at[slot], (sec, to_peer(1))
+        )
+
     def fp_copy(c, k):
         to = lax.rem(sec + k, sections)
         piece = lax.rem(to, 2)
@@ -589,8 +613,8 @@
         attention(1)
         mat = gathered(1, KV_HEADS - 1)
         final_sq = jnp.zeros((rows, 1), F32)
-        for c in range(chunks):
-            cols = slice(c * chunk, (c + 1) * chunk)
+        for c in range(parts):
+            cols = slice(c * cut, (c + 1) * cut)
             new = grown(1, mat, cols)
             xo[:, cols] = new
             final = new.astype(F32)
@@ -602,7 +626,7 @@
 
             @pl.when(sec == last)
             def _():
-                lanes = chunk // 128
+                lanes = cut // 128
                 row = jnp.concatenate(
                     [
                         final_v[c * lanes + i : c * lanes + i + 1, :].astype(F32)
@@ -611,16 +635,15 @@
                     axis=1,
                 )
                 both = (final * row).astype(BF16)
-                fin[0, me, c] = both[:half]
-                fin[1, me, c] = both[half:]
-                for k in range(1, sections):
-                    fp_copy(c, k).start()
-                for k in far_first:
-                    fin_copy(c, to_peer(k), me).start()
-                sib_copy(c, core, me).start()
+                fin[0, me, 0, :, cols] = both[:half]
+                fin[1, me, 0, :, cols] = both[half:]
 
         @pl.when(sec == last)
         def _():
+            for k in range(1, sections):
+                fp_copy(0, k).start()
+            fin_send()
+            sib_copy(0, core, me).start()
             fsq_in[me] = to_row(final_sq)
             for k in range(1, sections):
                 fp_sq(k).start()
@@ -635,8 +658,7 @@
             )
             with jax.named_scope("fp_wait"):
                 arriving.wait_recv()
-            for k in far_first:
-                fin_copy(c, to_peer(k), me).start()
+            fin_send()
 
             @pl.when(sec < last - 1)
             def _():
@@ -654,15 +676,24 @@
     def whole(piece, slot, send, recv):
         return remote(fin.at[piece, slot], fin.at[piece, slot], send, recv.at[slot], (sibling, me))
 
+    far = jnp.where(outer, 6, 4)
+    arrivals = [0, 1, far, 2, 3, 10 - far, 11 - far, far + 1]
+
+    def arriving_from(k):
+        return mate(me, arrivals[k] if relayed else k, n)[1]
+
     def pass_on(k):
-        _, peer = mate(me, k, n)
+        peer = arriving_from(k)
         with jax.named_scope("fin_wait"):
             whole(core, peer, fin_s, fin_r).wait_recv()
+        if relayed and k == 2:
+            side_copy(peer).start()
+
         for c in range(chunks):
             sib_copy(c, core, peer).start()
 
     def head(k, logits):
-        _, peer = mate(me, k, n)
+        peer = arriving_from(k)
         if isinstance(k, int) and k == 0:
 
             @pl.when(sec < last)
@@ -687,8 +718,14 @@
         pass_on(k)
         return head(k - lag, logits)
 
-    logits = lax.fori_loop(lag + 1, n, step, logits)
-    logits = lax.fori_loop(n - lag, n, head, logits)
+    if relayed:
+        for k in range(lag + 1, n):
+            logits = step(k, logits)
+        for k in range(n - lag, n):
+            logits = head(k, logits)
+    else:
+        logits = lax.fori_loop(lag + 1, n, step, logits)
+        logits = lax.fori_loop(n - lag, n, head, logits)
     all_fsq = remote(
         fsq_in.at[pl.ds(1, n - 1)], fsq_in.at[pl.ds(1, n - 1)], fsq_s, fsq_r, (sec, me)
     )
@@ -748,7 +785,16 @@
         for copy in help_copies:
             copy.wait_send()
 
-    sent(fin.at[0, others_n], fin_s)
+    if relayed:
+        sent(fin.at[0, pl.ds(0, n - 3)], fin_s)
+        sent(fin.at[0, 0], side_s)
+
+        @pl.when(jnp.logical_not(outer))
+        def _():
+            sent(fin.at[0, pl.ds(0, 2)], fin_s)
+
+    else:
+        sent(fin.at[0, others_n], fin_s)
     sent(fin.at[0, others_n], sib_s)
     all_fsq.wait_send()
 
@@ -827,12 +873,12 @@
     vm = pl.BlockSpec(memory_space=pltpu.VMEM)
     hbm = pl.BlockSpec(memory_space=pltpu.HBM)
     total = sections * n
-    chunks = 2
+    chunks = 1
     logprobs, chosen = pl.pallas_call(
         functools.partial(kernel, sections, n),
         out_shape=(
-            jax.ShapeDtypeStruct((rows, vocab), F32),
-            jax.ShapeDtypeStruct((1, 128), F32),
+            pltpu.VMEM((rows, vocab), F32),
+            pltpu.VMEM((1, 128), F32),
         ),
         in_specs=[hbm] * 12,
         out_specs=(vm, vm),
@@ -895,6 +941,7 @@
             dma,
             dma,
             dma((5,)),
+            dma,
         ],
         compiler_params=pltpu.CompilerParams(
             collective_id=0, has_side_effects=True, vmem_limit_bytes=60 * 1024 * 1024

time: 75.4 us -> 71.3 us (0.946)
  Pallas kernels: 72 us -> 69.3 us
  local copies, waits for them, and re-layouts: 2.57 us -> 1.13 us
    pallas_call x1, Pallas kernels: 72 us -> 69.3 us  [local(): pl.pallas_call(functools.partial(kernel, sections, n), out_shape=(pltpu.V...]
    unnamed x1, local copies, waits for them, and re-layouts: 1.42 us -> 0.62 us
where the time goes in v4:
time: 71.3 us; the launch traced here: 71.1 us
  Pallas kernels  69.3 us (97%)
  local copies, waits for them, and re-layouts  1.13 us (2%)
    pallas_call x1, Pallas kernels, local(): pl.pallas_call(functools.partial(kernel, sections, n), out_shape=(pltpu.V...  69.3 us

profile of v4, /device:TPU:0, one launch (start us, length us, event | category | flops | bytes accessed | tf_op | source)
XLA Modules:
  0.0 71.1 jit_solution(7514681206854381496)
XLA Ops:
  0.6 69.3 %shard_map.131 = (f32[32,384]{1,0:T(8,128)S(1)}, f32[1,128]{1,0:T(1,128)S(1)}) custom-call(bf16[32,1024]{1,0:T(8,128)(2,1)} %hidden.1, s32[1,32]{1,0:T(1,128)} %bitcast.7, s32[1,32]{1,0:T(1,128)} %bitcast.8, s32[1,32]{1,0:T(1,128)} %bitcast.9, bf16[1,1024]{1,0:T(2,128)(2,1)} %gain.1, bf16[1,1024,5120]{2,1,0:T(8,128)(2,1)} %qkv_weight.1, ...), custom_call_target="tpu_custom_call" | custom-call | tf_op jit(solution)/shard_map/pallas_call | solution.py:877
  70.0 0.6 copy.15
  70.6 0.5 slice_bitcast_fusion

commit v5 on v4

--- a/solution.py
+++ b/solution.py
@@ -130,7 +130,7 @@
     helps = (sec >= 2) & (core == 0)
     helped = (sec >= 2) & (core == 1)
     following = jnp.where(sec == 0, 1, sec + 2)
-    early = min(2, phases)
+    early = min(1, phases)
 
     def mate(own, k, count):
         if count & (count - 1):
@@ -148,7 +148,17 @@
         return other, other
 
     pairs = [mate(me, k, n) for k in range(n)]
-    far_first = range(n - 1, 0, -1)
+    across = max(d for d in range(1, n + 1) if n % d == 0 and d * d <= n)
+    relayed = across == 2 and n == 8
+    place = me // across
+    outer = (place == 0) | (place == n // across - 1)
+    far = jnp.where(outer, 6, 4)
+    if relayed:
+        far_peers = [
+            mate(me, k, n)[0] for k in (far + 1, far, 11 - far, 10 - far, 3, 2, 1)
+        ]
+    else:
+        far_peers = [pairs[k][0] for k in range(n - 1, 0, -1)]
 
     def to_peer(k):
         return pairs[k][0]
@@ -197,8 +207,8 @@
     hw_copy = pltpu.make_async_copy(head_weight, hw, w_sem.at[2])
 
     barrier = pltpu.get_barrier_semaphore()
-    for k in far_first:
-        pl.semaphore_signal(barrier, inc=1, device_id=(sec, to_peer(k)), device_id_type=MESH)
+    for peer in far_peers:
+        pl.semaphore_signal(barrier, inc=1, device_id=(sec, peer), device_id_type=MESH)
     for k in range(1, sections):
         pl.semaphore_signal(
             barrier, inc=1, device_id=(lax.rem(sec + k, sections), me), device_id_type=MESH
@@ -278,17 +288,15 @@
 
     def scale_rows(t):
         current = x[...].astype(F32)
-        sq[t] = jnp.broadcast_to(
-            to_row(jnp.sum(current * current, axis=1, keepdims=True)), sq.shape[1:]
-        )
+        sq[t] = to_row(jnp.sum(current * current, axis=1, keepdims=True))
         scaled[...] = (current * gain_v[t].astype(F32)).astype(BF16)
 
     def sq_copy(t, peer, slot):
         return remote(sq.at[t], sq_in.at[t, slot], sq_s.at[t], sq_r.at[t], (sec, peer))
 
     def sq_send(t):
-        for k in far_first:
-            sq_copy(t, to_peer(k), me).start()
+        for peer in far_peers:
+            sq_copy(t, peer, me).start()
         sq_in[t, me] = sq[t]
 
     def part_copy(t, phase, peer, slot):
@@ -313,8 +321,8 @@
             part[t, phase, p] = stage[p * span : (p + 1) * span, :].astype(BF16)
 
     def spread(t, phase):
-        for k in far_first:
-            part_copy(t, phase, to_peer(k), me).start()
+        for peer in far_peers:
+            part_copy(t, phase, peer, me).start()
         part_in[t, phase, me] = part[t, phase, me]
 
     def compute_only(k, carry):
@@ -419,7 +427,7 @@
             squares = squares + sq_in[t, p]
         factor = lax.rsqrt(
             jnp.sum(
-                jnp.where(own_lane == own_request, squares[0:1, :], 0.0), axis=1, keepdims=True
+                jnp.where(own_lane == own_request, squares, 0.0), axis=1, keepdims=True
             )
             / (n * width)
             + EPS
@@ -472,8 +480,8 @@
                 )
                 mixed = mixed + self_weight.astype(BF16).astype(F32) * value_new
                 att[t, h] = (mixed / denominator).astype(BF16)
-            for k in far_first:
-                att_copy(t, h, to_peer(k), me).start()
+            for peer in far_peers:
+                att_copy(t, h, peer, me).start()
             att_in[t, h, me] = att[t, h]
             return carry
 
@@ -573,11 +581,6 @@
         return remote(
             fsq_in.at[slot], fsq_in.at[slot], fsq_s, fsq_r, (sec, peer)
         )
-
-    across = max(d for d in range(1, n + 1) if n % d == 0 and d * d <= n)
-    relayed = across == 2 and n == 8
-    place = me // across
-    outer = (place == 0) | (place == n // across - 1)
 
     def fin_send():
         for k in (1, 6, 4, 5, 7, 2, 3) if relayed else range(1, n):
@@ -647,8 +650,8 @@
             fsq_in[me] = to_row(final_sq)
             for k in range(1, sections):
                 fp_sq(k).start()
-            for k in far_first:
-                fsq_copy(to_peer(k), me).start()
+            for peer in far_peers:
+                fsq_copy(peer, me).start()
 
     @pl.when(sec < last)
     def _():
@@ -668,15 +671,14 @@
             fsq_in.at[me], fsq_in.at[me], fq_s, fp_r.at[chunks], (last, me)
         )
         arriving.wait_recv()
-        for k in far_first:
-            fsq_copy(to_peer(k), me).start()
+        for peer in far_peers:
+            fsq_copy(peer, me).start()
 
     hw_copy.wait()
 
     def whole(piece, slot, send, recv):
         return remote(fin.at[piece, slot], fin.at[piece, slot], send, recv.at[slot], (sibling, me))
 
-    far = jnp.where(outer, 6, 4)
     arrivals = [0, 1, far, 2, 3, 10 - far, 11 - far, far + 1]
 
     def arriving_from(k):
@@ -893,8 +895,8 @@
             pltpu.VMEM((rows * group, HEAD_DIM), F32),
             pltpu.VMEM((2, phases, n, span, HEAD_DIM), BF16),
             pltpu.VMEM((2, phases, n, span, HEAD_DIM), BF16),
-            pltpu.VMEM((2, 8, 128), F32),
-            pltpu.VMEM((2, n, 8, 128), F32),
+            pltpu.VMEM((2, 1, 128), F32),
+            pltpu.VMEM((2, n, 1, 128), F32),
             pltpu.VMEM((2, 1, width), BF16),
             pltpu.VMEM((2, 1, qkv), BF16),
             pltpu.VMEM((width // 128, 128), BF16),

time: 71.3 us -> 70.5 us (0.989)
  Pallas kernels: 69.3 us -> 68.5 us
    pallas_call x1, Pallas kernels: 69.3 us -> 68.5 us  [local(): pl.pallas_call(functools.partial(kernel, sections, n), out_shape=(pltpu.V...]
where the time goes in v5:
time: 70.5 us; the launch traced here: 70.3 us
  Pallas kernels  68.5 us (97%)
  local copies, waits for them, and re-layouts  1.13 us (2%)
    pallas_call x1, Pallas kernels, local(): pl.pallas_call(functools.partial(kernel, sections, n), out_shape=(pltpu.V...  68.5 us

profile of v5, /device:TPU:0, one launch (start us, length us, event | category | flops | bytes accessed | tf_op | source)
XLA Modules:
  0.0 70.3 jit_solution(6299991672369512274)
XLA Ops:
  0.6 68.5 %shard_map.131 = (f32[32,384]{1,0:T(8,128)S(1)}, f32[1,128]{1,0:T(1,128)S(1)}) custom-call(bf16[32,1024]{1,0:T(8,128)(2,1)} %hidden.1, s32[1,32]{1,0:T(1,128)} %bitcast.7, s32[1,32]{1,0:T(1,128)} %bitcast.8, s32[1,32]{1,0:T(1,128)} %bitcast.9, bf16[1,1024]{1,0:T(2,128)(2,1)} %gain.1, bf16[1,1024,5120]{2,1,0:T(8,128)(2,1)} %qkv_weight.1, ...), custom_call_target="tpu_custom_call" | custom-call | tf_op jit(solution)/shard_map/pallas_call | solution.py:879
  69.2 0.6 copy.15
  69.8 0.5 slice_bitcast_fusion

commit v6 on v5

--- a/solution.py
+++ b/solution.py
@@ -121,7 +121,7 @@
     half = rows // 2
     chunks = fin.shape[2]
     chunk = width // chunks
-    parts = 2
+    parts = 1
     cut = width // parts
     core = lax.rem(sec, 2)
     sibling = sec + 1 - 2 * core

time: 70.5 us -> 70.1 us (level)
  no operation moved by 1% of the time
where the time goes in v6:
time: 70.1 us; the launch traced here: 69.9 us
  Pallas kernels  68.2 us (97%)
  local copies, waits for them, and re-layouts  1.13 us (2%)
    pallas_call x1, Pallas kernels, local(): pl.pallas_call(functools.partial(kernel, sections, n), out_shape=(pltpu.V...  68.2 us

profile of v6, /device:TPU:0, one launch (start us, length us, event | category | flops | bytes accessed | tf_op | source)
XLA Modules:
  0.0 69.9 jit_solution(6802210644527008037)
XLA Ops:
  0.6 68.2 %shard_map.131 = (f32[32,384]{1,0:T(8,128)S(1)}, f32[1,128]{1,0:T(1,128)S(1)}) custom-call(bf16[32,1024]{1,0:T(8,128)(2,1)} %hidden.1, s32[1,32]{1,0:T(1,128)} %bitcast.7, s32[1,32]{1,0:T(1,128)} %bitcast.8, s32[1,32]{1,0:T(1,128)} %bitcast.9, bf16[1,1024]{1,0:T(2,128)(2,1)} %gain.1, bf16[1,1024,5120]{2,1,0:T(8,128)(2,1)} %qkv_weight.1, ...), custom_call_target="tpu_custom_call" | custom-call | tf_op jit(solution)/shard_map/pallas_call | solution.py:879
  68.8 0.6 copy.15
  69.4 0.5 slice_bitcast_fusion
